TPU v7x, 1024 devices: a whole 4x4x32 slice. The times are simulated.
1024 devices in a mesh: seq: 32 (over y, z_hi, core), et: 32 (over z_lo, x).
Axes of the slice: x: 4, y: 4, z: 32 (z_hi: 4, z_lo: 8; z = z_hi * 8 + z_lo), core: 2. Of those that a mesh axis runs over, the one named last changes fastest.
Arguments:
- hidden_in: bfloat16 [1024, 4096], P('seq'), may hold values from -6 to 6
- expert_ids: int32 [1024, 2], P('seq'), may hold values from 0 to 7, all different within a row; in each aligned block of 32 rows (0 to 31, 32 to 63, ...) at most 10 rows name the same one
- gate_vals: bfloat16 [1024, 2], P('seq'), may hold values from 0 to 1, as said below
- w_gate: bfloat16 [32, 4096, 3584], P('et', None, 'seq'), may hold values from -0.09375 to 0.09375
- w_up: bfloat16 [32, 4096, 3584], P('et', None, 'seq'), may hold values from -0.09375 to 0.09375
- w_down: bfloat16 [32, 3584, 4096], P('et', 'seq'), may hold values from -0.09375 to 0.09375
Outputs:
- mixed: bfloat16 [1024, 4096], P('seq', 'et')
Inputs may be any that keep to these rules, and one draw needn't show every extreme that they name: `expert_ids`: the rows of each token name different experts; within each block of 32 rows (the rows of one device) no expert is named by more than 10 rows. `gate_vals`: each token's two weights sum to 1 up to bfloat16 rounding, the first is not the smaller.
All inputs are finite; a program needn't handle non-finite values.
Results may differ from a plain program's by a relative error of at most 0.019.
Values may be sent and summed in bfloat16 or wider, within the bound.
A program may use at most 32 MiB of HBM per device.

v0:
```python
import jax
import jax.numpy as jnp
from jax import lax
from jax.sharding import Mesh
from jax.sharding import PartitionSpec as P

EXPERTS = 8
SLOTS = 10
SEQ = ("seq_0", "seq_1", "seq_2")


def split_up(array, dim, count):
    before, after = (array.shape[:dim], array.shape[dim + 1 :])
    return jnp.moveaxis(array.reshape(*before, count, -1, *after), dim, 0)


def scatter_pairs(array, chips, core, dim):
    sizes = (lax.axis_size(chips), lax.axis_size(core))
    pieces = split_up(array, dim, sizes[0] * sizes[1])
    inside = pieces.shape[1:]
    pieces = pieces.reshape(*sizes, *inside).swapaxes(0, 1).reshape(-1, *inside)
    pieces = lax.psum_scatter(pieces, core, scatter_dimension=0, tiled=True)
    return lax.psum_scatter(pieces, chips, scatter_dimension=0, tiled=True)[0]


def sum_at_owner(array, axis, dim):
    count = lax.axis_size(axis)
    pieces = lax.all_to_all(split_up(array, dim, count), axis, 0, 0, tiled=True)
    return jnp.sum(pieces.astype(jnp.float32), axis=0)


def slot_numbers(routed):
    flattened = routed.reshape(-1)
    one_hot = (flattened[:, None] == jnp.arange(EXPERTS, dtype=jnp.int32)[None, :]).astype(
        jnp.int32
    )
    earlier = jnp.cumsum(one_hot, axis=0) - one_hot
    return jnp.sum(earlier * one_hot, axis=1).reshape(routed.shape)


def local(hidden_in, expert_ids, gate_vals, w_gate, w_up, w_down):
    group_size = lax.axis_size("et") // EXPERTS
    expert_here = lax.axis_index("et") // group_size
    slot_index = slot_numbers(expert_ids)
    chosen = expert_ids == expert_here
    columns = jnp.arange(SLOTS, dtype=jnp.int32)
    matches = chosen[:, None, :] & (slot_index[:, None, :] == columns[None, :, None])
    placing = jnp.any(matches, axis=2).astype(jnp.bfloat16)
    combining = jnp.sum(jnp.where(matches, gate_vals.astype(jnp.float32)[:, None, :], 0.0), axis=2)
    buffer = jnp.dot(placing.T, hidden_in, preferred_element_type=jnp.float32).astype(jnp.bfloat16)
    gate_local = w_gate[0]
    up_local = w_up[0]
    down_local = w_down[0]
    segment = lax.all_gather(buffer, SEQ, axis=0, tiled=True)
    gate_part = jnp.dot(segment, gate_local, preferred_element_type=jnp.float32)
    up_part = jnp.dot(segment, up_local, preferred_element_type=jnp.float32)
    activations = (jax.nn.silu(gate_part) * up_part).astype(jnp.bfloat16)
    partial_value = scatter_pairs(
        jnp.dot(activations, down_local, preferred_element_type=jnp.float32).astype(jnp.bfloat16),
        ("seq_0", "seq_1"),
        "seq_2",
        0,
    ).astype(jnp.float32)
    contribution = jnp.dot(combining, partial_value, precision=lax.Precision.HIGHEST)
    share_width = hidden_in.shape[1] // lax.axis_size("et")
    mixed_part = sum_at_owner(contribution.astype(jnp.bfloat16), "et", 1)
    residual_part = lax.dynamic_slice_in_dim(
        hidden_in, lax.axis_index("et") * share_width, share_width, 1
    )
    return (residual_part.astype(jnp.float32) + mixed_part).astype(jnp.bfloat16)


def solution(mesh):
    split = Mesh(mesh.devices.reshape(4, 4, 2, mesh.shape["et"]), ("seq_0", "seq_1", "seq_2", "et"))
    return jax.shard_map(
        local,
        mesh=split,
        in_specs=(
            P(SEQ, None),
            P(SEQ, None),
            P(SEQ, None),
            P("et", None, SEQ),
            P("et", None, SEQ),
            P("et", SEQ, None),
        ),
        out_specs=P(SEQ, "et"),
        check_vma=False,
    )
```

profile of v0, /device:TPU:24, one launch (start us, length us, event | category | flops | bytes accessed | tf_op | source)
XLA Modules:
  0.0 495.8 jit_solution(12885397509607810546)
XLA Ops:
  6.5 0.8 copy.24
  7.4 0.7 broadcast_compare_fusion
  8.1 0.1 eq.38
  8.2 0.1 fusion.15
  8.2 0.1 reduce_window_sum.11
  8.3 0.2 select_reduce_fusion
  8.5 0.1 eq.42
  8.6 0.1 copy.25
  8.7 1.8 fusion
  10.5 0.0 reduce-scatter.3.cloned.1.call-start
  10.6 182.3 %all-gather.3.cloned.1.call-done = bf16[32,10,4096]{2,1,0:T(8,128)(2,1)} async-done(((bf16[1,10,4096]{2,1,0:T(8,128)(2,1)}), bf16[32,10,4096]{2,1,0:T(8,128)(2,1)}) %all-gather.3.cloned.1.call-update) | async-done | bytes 2621456 | tf_op jit(solution)/shard_map/all_gather | solution.py:54
  192.8 3.3 reshape.13
  196.2 2.7 fusion.6
  198.8 5.6 %convolution_convert_fusion = bf16[320,4096]{1,0:T(8,128)(2,1)} fusion(bf16[320,4096]{1,0:T(8,128)(2,1)S(1)} %reshape.13, bf16[1,112,4096]{2,1,0:T(8,128)(2,1)S(1)} %copy-done, bf16[1,4096,112]{1,2,0:T(8,128)(2,1)} %param.10, f32[320,112]{1,0:T(8,128)} %fusion.6), kind=kOutput, calls=%fused_computation | convolution fusion | flops 588728320 | bytes 7221248 | tf_op jit(solution)/shard_map/dot_general | solution.py:59
  204.5 4.6 reshape_reshape.3
  209.1 5.2 %copy.27 = bf16[2,16,10,4096]{3,1,0,2:T(8,128)(2,1)} copy(bf16[2,16,10,4096]{3,2,0,1:T(8,128)(2,1)} %bitcast.30) | data formatting | bytes 5242880 | tf_op jit(solution)/shard_map/transpose | solution.py:21
  214.3 19.8 %reduce-scatter.3.cloned.1.call-done = bf16[16,10,4096]{2,0,1:T(8,128)(2,1)} async-done(((bf16[32,10,4096]{2,0,1:T(8,128)(2,1)}), bf16[16,10,4096]{2,0,1:T(8,128)(2,1)}) %reduce-scatter.3.cloned.1.call-update) | async-done | bytes 1310736 | tf_op jit(solution)/shard_map/reduce_scatter | solution.py:22
  234.1 3.5 copy.28
  237.7 219.5 %reduce-scatter.5.cloned.1.call-done = bf16[1,10,4096]{2,1,0:T(8,128)(2,1)} async-done(((bf16[16,10,4096]{2,1,0:T(8,128)(2,1)}), bf16[1,10,4096]{2,1,0:T(8,128)(2,1)}) %reduce-scatter.5.cloned.1.call-update) | async-done | bytes 81936 | tf_op jit(solution)/shard_map/reduce_scatter | solution.py:23
  457.2 1.3 fusion.1
  458.5 0.7 copy.33
  459.2 11.9 %all-to-all-start = ((bf16[32,32,128]{2,1,0:T(8,128)(2,1)}), bf16[32,32,128]{2,1,0:T(8,128)(2,1)S(1)}, u32[]{:S(2)}, u32[]{:S(2)}) async-start(bf16[32,32,128]{2,1,0:T(8,128)(2,1)} %bitcast.29), calls=%async_computation.2 | async-start | bytes 524288 | tf_op jit(solution)/shard_map/all_to_all | solution.py:28
  471.2 16.8 %all-to-all-done = bf16[32,32,128]{2,1,0:T(8,128)(2,1)S(1)} async-done(((bf16[32,32,128]{2,1,0:T(8,128)(2,1)}), bf16[32,32,128]{2,1,0:T(8,128)(2,1)S(1)}, u32[]{:S(2)}, u32[]{:S(2)}) %all-to-all-start) | async-done | bytes 262176 | tf_op jit(solution)/shard_map/all_to_all | solution.py:28
  488.0 1.3 add_convert_fusion
  (13 shorter events, 0.2 us)
Async XLA Ops:
  6.5 192.3 %copy-start = (bf16[1,112,4096]{2,1,0:T(8,128)(2,1)S(1)}, bf16[1,112,4096]{2,1,0:T(8,128)(2,1)}, u32[]{:S(2)}) copy-start(bf16[1,112,4096]{2,1,0:T(8,128)(2,1)} %param.11) | copy-start | bytes 2752516
  6.5 186.3 %all-gather.3.cloned.1.call-start = ((), (), s32[]{:S(2)}) async-start(), calls=%async_computation.5 | async-start | bytes 4325376 | tf_op jit(solution)/shard_map/all_gather | solution.py:54
  10.5 223.6 %reduce-scatter.3.cloned.1.call-start = ((), (), s32[]{:S(2)}) async-start(), calls=%async_computation.3 | async-start | bytes 3932160 | tf_op jit(solution)/shard_map/reduce_scatter | solution.py:22
  214.3 23.4 %copy-start.1 = (bf16[32,2]{0,1:T(2,128)(2,1)S(1)}, bf16[32,2]{0,1:T(2,128)(2,1)}, u32[]{:S(2)}) copy-start(bf16[32,2]{0,1:T(2,128)(2,1)} %param.8) | copy-start | bytes 388
  214.3 242.9 %reduce-scatter.5.cloned.1.call-start = ((), (), s32[]{:S(2)}) async-start(), calls=%async_computation.4 | async-start | bytes 2228224 | tf_op jit(solution)/shard_map/reduce_scatter | solution.py:23
  459.2 28.7 %all-to-all-start = ((bf16[32,32,128]{2,1,0:T(8,128)(2,1)}), bf16[32,32,128]{2,1,0:T(8,128)(2,1)S(1)}, u32[]{:S(2)}, u32[]{:S(2)}) async-start(bf16[32,32,128]{2,1,0:T(8,128)(2,1)} %bitcast.29), calls=%async_computation.2 | async-start | bytes 524288 | tf_op jit(solution)/shard_map/all_to_all | solution.py:28
Sparse Core Ops, SparseCore 0:
  11.6 181.1 all-gather.2
  214.4 19.7 reduce-scatter.2
  239.4 217.7 reduce-scatter.4
where the time goes:
time: 497 us; the launch traced here: 496 us
  waiting for transfers between devices  438 us (88%)
  local copies, waits for them, and re-layouts  18.4 us (4%)
  between operations  13.2 us (3%)
  starting transfers between devices  12 us (2%)
  matrix products  11.4 us (2%)
    reduce_scatter x1, waiting for transfers between devices, scatter_pairs(): return lax.psum_scatter(pieces, chips, scatter_dimension=0, tiled=True)[0]  220 us
    all_gather x1, waiting for transfers between devices, local(): segment = lax.all_gather(buffer, SEQ, axis=0, tiled=True)  182 us
    reduce_scatter x1, waiting for transfers between devices, scatter_pairs(): pieces = lax.psum_scatter(pieces, core, scatter_dimension=0, tiled=True)  19.8 us
    all_to_all x1, waiting for transfers between devices, sum_at_owner(): pieces = lax.all_to_all(split_up(array, dim, count), axis, 0, 0, tiled=True)  16.8 us
    all_to_all x1, starting transfers between devices, sum_at_owner(): pieces = lax.all_to_all(split_up(array, dim, count), axis, 0, 0, tiled=True)  11.9 us
  transfers between devices with their start and end apart: 4, of which 4 were waited for; matrix products, arithmetic and copies ran while one was open for 0% of the time, Pallas kernels for 0%

commit v1 on v0

v1 whole, which is shorter than its diff:
```python
import functools

import jax
import jax.numpy as jnp
from jax import lax
from jax.experimental import pallas as pl
from jax.experimental.pallas import tpu as pltpu
from jax.sharding import Mesh
from jax.sharding import PartitionSpec as P

EXPERTS = 8
SLOTS = 10
PAIRS = SLOTS // 2
LANES = 128
AXES = ("y", "zh", "c", "zl", "x")
NY, NZH, NC, NZL, NX = 4, 4, 2, 8, 4
SEQ = ("y", "zh", "c")
ET = ("zl", "x")
ROWS = NY * NC * SLOTS
MESH = pl.DeviceIdType.MESH


def moe_kernel(
    hidden_any, ids_ref, gate_ref, wg_any, wu_any, wd_any,
    out_ref,
    hid, wgu, wd, picked, gathered, xbuf, ysend, yrecv, yown, rrecv, total, homeward, arrived, returned,
    load_sem, disp_send, disp_recv, ag_send, ag_recv, fwd_send, fwd_recv,
    pair_send, pair_recv, rs_send, rs_recv, ret_send, ret_recv,
):
    at = {name: lax.axis_index(name) for name in AXES}
    y, zh, c, zl, x = (at[name] for name in AXES)

    def device(**other):
        return {**at, **other}

    def remote(src, dst, send, recv, dev):
        return pltpu.make_async_remote_copy(
            src_ref=src, dst_ref=dst, send_sem=send, recv_sem=recv, device_id=dev, device_id_type=MESH
        )

    def up(v, d, n):
        return lax.rem(v + d, n)

    barrier = pltpu.get_barrier_semaphore()

    def hello(**other):
        pl.semaphore_signal(barrier, inc=1, device_id=device(**other), device_id_type=MESH)

    def hello_plane(p, carry):
        hello(x=up(x, lax.rem(p, NX), NX), y=up(y, p // NX, NY))
        return carry

    def hello_far(p, carry):
        hello(y=up(y, lax.rem(p, NY), NY), c=up(c, p // NY, NC), zh=up(zh, 1, NZH))
        hello(y=up(y, lax.rem(p, NY), NY), c=up(c, p // NY, NC), zh=up(zh, 3, NZH))
        return carry

    def hello_region(p, carry):
        hello(zl=up(zl, p, NZL))
        return carry

    def hello_twin(p, carry):
        hello(y=up(y, p, NY), c=1 - c)
        return carry

    lax.fori_loop(0, NY * NC, hello_far, 0)
    lax.fori_loop(1, NZL, hello_region, 0)
    lax.fori_loop(1, NX * NY, hello_plane, 0)
    lax.fori_loop(0, NY, hello_twin, 0)

    loads = [
        pltpu.make_async_copy(hidden_any, hid, load_sem.at[0]),
        pltpu.make_async_copy(wg_any, wgu.at[pl.ds(0, 112)], load_sem.at[1]),
        pltpu.make_async_copy(wu_any, wgu.at[pl.ds(128, 112)], load_sem.at[2]),
        pltpu.make_async_copy(wd_any, wd.at[pl.ds(0, 112)], load_sem.at[3]),
    ]
    for load in loads:
        load.start()
    width = wd.shape[1]
    wgu[pl.ds(112, 16), :] = jnp.zeros((16, width), jnp.bfloat16)
    wgu[pl.ds(240, 16), :] = jnp.zeros((16, width), jnp.bfloat16)
    wd[pl.ds(112, 16), :] = jnp.zeros((16, width), jnp.bfloat16)

    tokens = ids_ref.shape[1]
    ids = ids_ref[...]
    expert = lax.broadcasted_iota(jnp.int32, (EXPERTS, tokens), 0)
    first, second = ids[0:1, :], ids[1:2, :]
    named = (jnp.where(first == expert, 1.0, 0.0) + jnp.where(second == expert, 1.0, 0.0)).astype(jnp.float32)
    before = jnp.where(
        lax.broadcasted_iota(jnp.int32, (tokens, tokens), 0) < lax.broadcasted_iota(jnp.int32, (tokens, tokens), 1),
        1.0, 0.0,
    ).astype(jnp.float32)
    earlier = jnp.dot(named, before, preferred_element_type=jnp.float32)

    def number(chosen):
        slot = jnp.sum(jnp.where(chosen == expert, earlier, 0.0), axis=0, keepdims=True)
        return chosen * SLOTS + slot.astype(jnp.int32)

    n_first, n_second = number(first), number(second)
    wanted = lax.broadcasted_iota(jnp.int32, (16, tokens), 0)
    wanted = jnp.where(wanted < SLOTS, wanted + zl * SLOTS, -1)
    placing = (
        jnp.where(n_first == wanted, 1.0, 0.0) + jnp.where(n_second == wanted, 1.0, 0.0)
    ).astype(jnp.bfloat16)
    loads[0].wait()
    for j in range(NZL):
        block = hid[:, pl.ds(pl.multiple_of((j * NX + x) * LANES, LANES), LANES)]
        rows = jnp.dot(placing, block, preferred_element_type=jnp.float32)
        for p in range(PAIRS):
            picked[j, p] = rows[2 * p : 2 * p + 2].astype(jnp.bfloat16)

    me = y * NC + c
    pl.semaphore_wait(barrier, 2 * NY * NC + (NZL - 1) + (NX * NY - 1) + NY)

    def to_region(step, group):
        def send(p, carry):
            ty, tc = up(y, lax.rem(p, NY), NY), up(c, p // NY, NC)
            remote(
                picked.at[ty * NC + tc], gathered.at[group, me], disp_send, disp_recv.at[group],
                device(y=ty, c=tc, zh=up(zh, step, NZH)),
            ).start()
            return carry
        return send

    lax.fori_loop(0, NY * NC, to_region(3, 1), 0)
    lax.fori_loop(0, NY * NC, to_region(1, 2), 0)
    lax.fori_loop(1, NY * NC, to_region(0, 0), 0)
    gathered[0, me] = picked[me]

    def mine(group):
        return xbuf.at[group, :, pl.ds(pl.multiple_of((me * NX + x) * LANES, LANES), LANES)]

    def spread(group):
        dst = mine(group)
        for s in range(NY * NC):
            for p in range(PAIRS):
                dst[pl.ds((s * PAIRS + p) * 2, 2), :] = gathered[group, s, p]

        def send(p, carry):
            remote(
                mine(group), mine(group), ag_send, ag_recv.at[group],
                device(x=up(x, lax.rem(p, NX), NX), y=up(y, p // NX, NY)),
            ).start()
            return carry

        lax.fori_loop(1, NX * NY, send, 0)

    def waits(ref, sem):
        pltpu.make_async_copy(ref, ref, sem).wait()

    def run(group, half, ty):
        return xbuf.at[group, :, pl.ds(pl.multiple_of((ty * NC + half) * NX * LANES, LANES), NX * LANES)]

    def forward(group):
        waits(xbuf.at[group, :, pl.ds(0, 15 * LANES)], ag_recv.at[group])
        for ty in range(NY):
            remote(run(group, c, ty), run(group, c, ty), fwd_send, fwd_recv.at[group], device(c=1 - c)).start()

    def compute(group):
        waits(xbuf.at[group, :, pl.ds(0, 16 * LANES)], fwd_recv.at[group])
        h = lax.dot_general(
            xbuf[group], wgu[...], (((1,), (1,)), ((), ())), preferred_element_type=jnp.float32
        )
        g, u = h[:, :128], h[:, 128:]
        act = (g / (1.0 + jnp.exp(-g)) * u).astype(jnp.bfloat16)

        def down(half, ty):
            cols = pl.ds(pl.multiple_of((ty * NC + half) * NX * LANES, LANES), NX * LANES)
            return jnp.dot(act, wd[:, cols], preferred_element_type=jnp.float32)

        for ty in range(NY):
            ysend[group, ty] = down(1 - c, ty).astype(jnp.bfloat16)
            remote(ysend.at[group, ty], yrecv.at[group, ty], pair_send, pair_recv.at[group], device(c=1 - c)).start()
        for ty in range(NY):
            yown[group, ty] = down(c, ty).astype(jnp.bfloat16)

    def scatter(group):
        waits(yrecv.at[group], pair_recv.at[group])
        for ty in range(NY):
            both = yown[group, ty].astype(jnp.float32) + yrecv[group, ty].astype(jnp.float32)
            yown[group, ty] = both.astype(jnp.bfloat16)

        def send(p, carry):
            tx, ty = up(x, lax.rem(p, NX), NX), up(y, p // NX, NY)
            remote(
                yown.at[group, ty, :, pl.ds(pl.multiple_of(tx * LANES, LANES), LANES)],
                rrecv.at[group, p - 1], rs_send, rs_recv.at[group], device(x=tx, y=ty),
            ).start()
            return carry

        lax.fori_loop(1, NX * NY, send, 0)

    def send_home(group, step):
        waits(rrecv.at[group], rs_recv.at[group])
        acc = yown[group, y, :, pl.ds(pl.multiple_of(x * LANES, LANES), LANES)].astype(jnp.float32)
        for s in range(NX * NY - 1):
            acc = acc + rrecv[group, s].astype(jnp.float32)
        total[...] = acc
        for s in range(NY * NC):
            for p in range(PAIRS):
                homeward[group, s, p] = total[pl.ds((s * PAIRS + p) * 2, 2), :].astype(jnp.bfloat16)
        target_zh = up(zh, step, NZH)

        def send(s, carry):
            ty, tc = s // NC, lax.rem(s, NC)
            dst = arrived.at[zh, zl]
            here = (target_zh == zh) & (ty == y) & (tc == c) & (zl == me)

            @pl.when(here)
            def _():
                pltpu.make_async_copy(homeward.at[group, s], dst, ret_recv).start()

            @pl.when(jnp.logical_not(here))
            def _():
                remote(
                    homeward.at[group, s], dst, ret_send, ret_recv,
                    device(y=ty, c=tc, zh=target_zh, zl=me),
                ).start()
            return carry

        lax.fori_loop(0, NY * NC, send, 0)

    waits(gathered.at[0, pl.ds(0, 7)], disp_recv.at[0])
    spread(0)
    forward(0)
    waits(gathered.at[1], disp_recv.at[1])
    remote(
        gathered.at[1, pl.ds(0, 4)], gathered.at[3, pl.ds(0, 4)], disp_send, disp_recv.at[3],
        device(zh=up(zh, 3, NZH)),
    ).start()
    waits(gathered.at[2], disp_recv.at[2])
    remote(
        gathered.at[2, pl.ds(4, 4)], gathered.at[3, pl.ds(4, 4)], disp_send, disp_recv.at[3],
        device(zh=up(zh, 1, NZH)),
    ).start()
    spread(1)
    spread(2)
    for load in loads[1:]:
        load.wait()
    compute(0)
    forward(1)
    scatter(0)
    waits(gathered.at[3], disp_recv.at[3])
    spread(3)
    forward(2)
    compute(1)
    compute(2)
    forward(3)
    scatter(1)
    scatter(2)
    compute(3)
    send_home(0, 0)
    scatter(3)
    send_home(1, 1)
    send_home(2, 3)
    send_home(3, 2)

    waits(arrived, ret_recv)
    for e in range(EXPERTS):
        for p in range(PAIRS):
            part = arrived[0, e, p].astype(jnp.float32)
            for k in range(1, NZH):
                part = part + arrived[k, e, p].astype(jnp.float32)
            returned[pl.ds((e * PAIRS + p) * 2, 2), :] = part
    place = lax.broadcasted_iota(jnp.int32, (EXPERTS * SLOTS, tokens), 0)
    gates = gate_ref[...].astype(jnp.float32)
    combining = jnp.where(n_first == place, gates[0:1, :], 0.0) + jnp.where(n_second == place, gates[1:2, :], 0.0)
    mixed = lax.dot_general(
        combining, returned[...], (((0,), (0,)), ((), ())),
        preferred_element_type=jnp.float32, precision=lax.Precision.HIGHEST,
    )
    residual = hid[:, pl.ds(pl.multiple_of((zl * NX + x) * LANES, LANES), LANES)].astype(jnp.float32)
    out_ref[...] = (residual + mixed).astype(jnp.bfloat16)

    for _ in range(3):
        waits(gathered.at[1], disp_send)
    waits(gathered.at[0, pl.ds(0, 7)], disp_send)
    for group in range(4):
        waits(xbuf.at[group, :, pl.ds(0, 15 * LANES)], ag_send)
        waits(xbuf.at[group, :, pl.ds(0, 16 * LANES)], fwd_send)
        waits(yrecv.at[group], pair_send)
        waits(rrecv.at[group], rs_send)
    waits(arrived.at[pl.ds(0, 3)], ret_send)
    waits(arrived.at[3, pl.ds(0, 7)], ret_send)

    @pl.when(zl != me)
    def _():
        waits(arrived.at[3, 7], ret_send)


def local(hidden_in, expert_ids, gate_vals, w_gate, w_up, w_down):
    tokens, width = hidden_in.shape
    ids = jnp.swapaxes(expert_ids, 0, 1)
    gates = jnp.swapaxes(gate_vals, 0, 1)
    wg = jnp.swapaxes(w_gate[0], 0, 1)
    wu = jnp.swapaxes(w_up[0], 0, 1)
    bf16, f32 = jnp.bfloat16, jnp.float32
    dma, anywhere, vmem = pltpu.SemaphoreType.DMA, pl.BlockSpec(memory_space=pl.ANY), pl.BlockSpec(memory_space=pltpu.VMEM)
    return pl.pallas_call(
        moe_kernel,
        name="moe",
        out_shape=jax.ShapeDtypeStruct((tokens, LANES), bf16),
        in_specs=[anywhere, vmem, vmem, anywhere, anywhere, anywhere],
        out_specs=vmem,
        scratch_shapes=[
            pltpu.VMEM((tokens, width), bf16),
            pltpu.VMEM((256, width), bf16),
            pltpu.VMEM((128, width), bf16),
            pltpu.VMEM((8, PAIRS, 2, LANES), bf16),
            pltpu.VMEM((4, 8, PAIRS, 2, LANES), bf16),
            pltpu.VMEM((4, ROWS, width), bf16),
            pltpu.VMEM((4, NY, ROWS, NX * LANES), bf16),
            pltpu.VMEM((4, NY, ROWS, NX * LANES), bf16),
            pltpu.VMEM((4, NY, ROWS, NX * LANES), bf16),
            pltpu.VMEM((4, NX * NY - 1, ROWS, LANES), bf16),
            pltpu.VMEM((ROWS, LANES), f32),
            pltpu.VMEM((4, 8, PAIRS, 2, LANES), bf16),
            pltpu.VMEM((4, 8, PAIRS, 2, LANES), bf16),
            pltpu.VMEM((ROWS, LANES), f32),
            dma((4,)), dma, dma((4,)), dma, dma((4,)), dma, dma((4,)),
            dma, dma((4,)), dma, dma((4,)), dma, dma,
        ],
        compiler_params=pltpu.CompilerParams(
            collective_id=0, has_side_effects=True, vmem_limit_bytes=40 * 1024 * 1024
        ),
    )(hidden_in, ids, gates, wg, wu, w_down[0])


def solution(mesh):
    split = Mesh(mesh.devices.reshape(NY, NZH, NC, NZL, NX), AXES)
    return jax.shard_map(
        local,
        mesh=split,
        in_specs=(
            P(SEQ, None),
            P(SEQ, None),
            P(SEQ, None),
            P(ET, None, SEQ),
            P(ET, None, SEQ),
            P(ET, SEQ, None),
        ),
        out_specs=P(SEQ, ET),
        check_vma=False,
    )
```

time: 497 us -> 88.3 us (0.18)
  waiting for transfers between devices: 438 us -> 0 us
  Pallas kernels: 0 us -> 80.8 us
  between operations: 13.2 us -> 0.02 us
  local copies, waits for them, and re-layouts: 18.4 us -> 5.77 us
  starting transfers between devices: 12 us -> 0 us
  matrix products: 11.4 us -> 0 us
    reduce_scatter x2 -> x0, waiting for transfers between devices: 239 us -> none  [the longest x1 220 us: scatter_pairs(): return lax.psum_scatter(pieces, chips, scatter_dimension=0, tiled=True)[0]]
    all_gather x1 -> x0, waiting for transfers between devices: 182 us -> none  [local(): segment = lax.all_gather(buffer, SEQ, axis=0, tiled=True)]
    pallas_call x0 -> x1, Pallas kernels: none -> 80.8 us  [local(): pl.pallas_call(moe_kernel, name='moe', out_shape=jax.ShapeDtypeStruct((to...]
    all_to_all x1 -> x0, waiting for transfers between devices: 16.8 us -> none  [sum_at_owner(): pieces = lax.all_to_all(split_up(array, dim, count), axis, 0, 0, tiled=True)]
    all_to_all x1 -> x0, starting transfers between devices: 11.9 us -> none  [sum_at_owner(): pieces = lax.all_to_all(split_up(array, dim, count), axis, 0, 0, tiled=True)]
    dot_general x4 -> x0, matrix products: 11.4 us -> none  [the longest x1 5.62 us: local(): jnp.dot(activations, down_local, preferred_element_type=jnp.float32)]
    transpose x1 -> x0, local copies, waits for them, and re-layouts: 5.15 us -> none  [scatter_pairs(): pieces = pieces.reshape(*sizes, *inside).swapaxes(0, 1).reshape(-1, *inside)]
  transfers between devices with their start and end apart: 4 -> 0, of which waited for: 4 -> 0; matrix products, arithmetic and copies ran while one was open for 0% -> 0% of each run, Pallas kernels for 0% -> 0%
where the time goes in v1:
time: 88.3 us; the launch traced here: 86.6 us
  Pallas kernels  80.8 us (92%)
  local copies, waits for them, and re-layouts  5.77 us (7%)
    pallas_call x1, Pallas kernels, local(): pl.pallas_call(moe_kernel, name='moe', out_shape=jax.ShapeDtypeStruct((to...  80.8 us
    unnamed x13, local copies, waits for them, and re-layouts  5.77 us

profile of v1, /device:TPU:24, one launch (start us, length us, event | category | flops | bytes accessed | tf_op | source)
XLA Modules:
  0.0 86.6 jit_solution(2315051085949404110)
XLA Ops:
  0.0 0.0 copy-start.4
  0.0 0.0 copy-start.5
  0.0 0.7 copy-done.4
  0.7 0.0 copy-done.5
  0.7 0.0 copy-start
  0.7 1.2 %copy-done = bf16[1,4096,112]{1,2,0:T(8,128)(2,1)S(1)} copy-done((bf16[1,4096,112]{1,2,0:T(8,128)(2,1)S(1)}, bf16[1,4096,112]{1,2,0:T(8,128)(2,1)}, u32[]{:S(2)}) %copy-start) | copy-done | bytes 917528
  1.9 0.0 copy-start.1
  1.9 1.2 %copy-done.1 = bf16[1,4096,112]{1,2,0:T(8,128)(2,1)S(1)} copy-done((bf16[1,4096,112]{1,2,0:T(8,128)(2,1)S(1)}, bf16[1,4096,112]{1,2,0:T(8,128)(2,1)}, u32[]{:S(2)}) %copy-start.1) | copy-done | bytes 917528
  3.0 0.0 copy-start.2
  3.0 1.2 %copy-done.2 = bf16[1,112,4096]{2,1,0:T(8,128)(2,1)S(1)} copy-done((bf16[1,112,4096]{2,1,0:T(8,128)(2,1)S(1)}, bf16[1,112,4096]{2,1,0:T(8,128)(2,1)}, u32[]{:S(2)}) %copy-start.2) | copy-done | bytes 917528
  4.2 0.0 copy-start.3
  4.2 0.9 %copy-done.3 = bf16[32,4096]{1,0:T(8,128)(2,1)S(1)} copy-done((bf16[32,4096]{1,0:T(8,128)(2,1)S(1)}, bf16[32,4096]{1,0:T(8,128)(2,1)}, u32[]{:S(2)}) %copy-start.3) | copy-done | bytes 262168
  5.2 80.8 %moe.1 = bf16[32,128]{1,0:T(8,128)(2,1)S(1)} custom-call(bf16[32,4096]{1,0:T(8,128)(2,1)S(1)} %copy-done.3, s32[2,32]{1,0:T(2,128)S(1)} %bitcast.12, bf16[2,32]{1,0:T(2,128)(2,1)S(1)} %bitcast.13, bf16[112,4096]{1,0:T(8,128)(2,1)S(1)} %bitcast.9, bf16[112,4096]{1,0:T(8,128)(2,1)S(1)} %bitcast.10, bf16[112,4096]{1,0:T(8,128)(2,1)S(1)} %bitcast.11), custom_call_target="tpu_custom_call" | custom-call | tf_op jit(solution)/shard_map/moe/pallas_call | solution.py:299
  86.0 0.6 copy.8
Async XLA Ops:
  0.0 0.7 copy-start.4
  0.0 0.7 copy-start.5
  0.7 1.2 %copy-start = (bf16[1,4096,112]{1,2,0:T(8,128)(2,1)S(1)}, bf16[1,4096,112]{1,2,0:T(8,128)(2,1)}, u32[]{:S(2)}) copy-start(bf16[1,4096,112]{1,2,0:T(8,128)(2,1)} %param.9) | copy-start | bytes 2752516
  1.9 1.2 %copy-start.1 = (bf16[1,4096,112]{1,2,0:T(8,128)(2,1)S(1)}, bf16[1,4096,112]{1,2,0:T(8,128)(2,1)}, u32[]{:S(2)}) copy-start(bf16[1,4096,112]{1,2,0:T(8,128)(2,1)} %param.10) | copy-start | bytes 2752516
  3.0 1.2 %copy-start.2 = (bf16[1,112,4096]{2,1,0:T(8,128)(2,1)S(1)}, bf16[1,112,4096]{2,1,0:T(8,128)(2,1)}, u32[]{:S(2)}) copy-start(bf16[1,112,4096]{2,1,0:T(8,128)(2,1)} %param.11) | copy-start | bytes 2752516
  4.2 0.9 %copy-start.3 = (bf16[32,4096]{1,0:T(8,128)(2,1)S(1)}, bf16[32,4096]{1,0:T(8,128)(2,1)}, u32[]{:S(2)}) copy-start(bf16[32,4096]{1,0:T(8,128)(2,1)} %hidden_any.1) | copy-start | bytes 786436

commit v2 on v1

v2 whole, which is shorter than its diff:
```python
import functools

import jax
import jax.numpy as jnp
from jax import lax
from jax.experimental import pallas as pl
from jax.experimental.pallas import tpu as pltpu
from jax.sharding import Mesh
from jax.sharding import PartitionSpec as P

EXPERTS = 8
SLOTS = 10
PAIRS = SLOTS // 2
LANES = 128
AXES = ("y", "zh", "c", "zl", "x")
NY, NZH, NC, NZL, NX = 4, 4, 2, 8, 4
SEQ = ("y", "zh", "c")
ET = ("zl", "x")
ROWS = NY * NC * SLOTS
MESH = pl.DeviceIdType.MESH


def moe_kernel(
    hidden_any, ids_any, gate_any, wg_any, wu_any, wd_any,
    out_ref,
    hid, ids_ref, gate_ref, wgu, wd, picked, gathered, xbuf, ysend, yrecv, yown, rrecv, total, homeward, arrived, returned,
    load_sem, disp_send, disp_recv, ag_send, ag_recv, fwd_send, fwd_recv,
    pair_send, pair_recv, rs_send, rs_recv, ret_send, ret_recv,
):
    scope = jax.named_scope
    at = {name: lax.axis_index(name) for name in AXES}
    y, zh, c, zl, x = (at[name] for name in AXES)

    def device(**other):
        return {**at, **other}

    def remote(src, dst, send, recv, dev):
        return pltpu.make_async_remote_copy(
            src_ref=src, dst_ref=dst, send_sem=send, recv_sem=recv, device_id=dev, device_id_type=MESH
        )

    def waits(ref, sem):
        pltpu.make_async_copy(ref, ref, sem).wait()

    def up(v, d, n):
        return lax.rem(v + d, n)

    barrier = pltpu.get_barrier_semaphore()

    def hello(**other):
        pl.semaphore_signal(barrier, inc=1, device_id=device(**other), device_id_type=MESH)

    def hello_plane(p, carry):
        hello(x=up(x, lax.rem(p, NX), NX), y=up(y, p // NX, NY))
        return carry

    def hello_far(p, carry):
        hello(y=up(y, lax.rem(p, NY), NY), c=up(c, p // NY, NC), zh=up(zh, 1, NZH))
        hello(y=up(y, lax.rem(p, NY), NY), c=up(c, p // NY, NC), zh=up(zh, 3, NZH))
        return carry

    def hello_region(p, carry):
        hello(zl=up(zl, p, NZL))
        return carry

    def hello_twin(p, carry):
        hello(y=up(y, p, NY), c=1 - c)
        return carry

    lax.fori_loop(0, NY * NC, hello_far, 0)
    lax.fori_loop(1, NZL, hello_region, 0)
    lax.fori_loop(1, NX * NY, hello_plane, 0)
    lax.fori_loop(0, NY, hello_twin, 0)

    loads = [
        pltpu.make_async_copy(ids_any, ids_ref, load_sem.at[4]),
        pltpu.make_async_copy(gate_any, gate_ref, load_sem.at[5]),
        pltpu.make_async_copy(hidden_any, hid, load_sem.at[0]),
        pltpu.make_async_copy(wg_any, wgu.at[pl.ds(0, 112)], load_sem.at[1]),
        pltpu.make_async_copy(wu_any, wgu.at[pl.ds(128, 112)], load_sem.at[2]),
        pltpu.make_async_copy(wd_any, wd.at[pl.ds(0, 112)], load_sem.at[3]),
    ]
    for load in loads:
        load.start()
    width = wd.shape[1]
    wgu[pl.ds(112, 16), :] = jnp.zeros((16, width), jnp.bfloat16)
    wgu[pl.ds(240, 16), :] = jnp.zeros((16, width), jnp.bfloat16)
    wd[pl.ds(112, 16), :] = jnp.zeros((16, width), jnp.bfloat16)
    loads[0].wait()
    loads[1].wait()

    tokens = ids_ref.shape[1]
    ids = ids_ref[...]
    expert = lax.broadcasted_iota(jnp.int32, (EXPERTS, tokens), 0)
    first, second = ids[0:1, :], ids[1:2, :]
    named = (jnp.where(first == expert, 1.0, 0.0) + jnp.where(second == expert, 1.0, 0.0)).astype(jnp.float32)
    before = jnp.where(
        lax.broadcasted_iota(jnp.int32, (tokens, tokens), 0) < lax.broadcasted_iota(jnp.int32, (tokens, tokens), 1),
        1.0, 0.0,
    ).astype(jnp.float32)
    earlier = jnp.dot(named, before, preferred_element_type=jnp.float32)

    def number(chosen):
        slot = jnp.sum(jnp.where(chosen == expert, earlier, 0.0), axis=0, keepdims=True)
        return chosen * SLOTS + slot.astype(jnp.int32)

    n_first, n_second = number(first), number(second)
    wanted = lax.broadcasted_iota(jnp.int32, (16, tokens), 0)
    wanted = jnp.where(wanted < SLOTS, wanted + zl * SLOTS, -1)
    placing = (
        jnp.where(n_first == wanted, 1.0, 0.0) + jnp.where(n_second == wanted, 1.0, 0.0)
    ).astype(jnp.bfloat16)
    loads[2].wait()
    for j in range(NZL):
        block = hid[:, pl.ds(pl.multiple_of((j * NX + x) * LANES, LANES), LANES)]
        rows = jnp.dot(placing, block, preferred_element_type=jnp.float32)
        for p in range(PAIRS):
            picked[j, p] = rows[2 * p : 2 * p + 2].astype(jnp.bfloat16)

    me = y * NC + c
    with scope("w_barrier"):
        pl.semaphore_wait(barrier, 2 * NY * NC + (NZL - 1) + (NX * NY - 1) + NY)

    order = (
        zh,
        jnp.where(zh == 0, 1, 0),
        jnp.where(zh == 0, 3, jnp.where(zh == 1, 2, 1)),
        jnp.where((zh == 1) | (zh == 2), 3, 2),
    )
    ahead, behind, across = up(zh, 1, NZH), up(zh, 3, NZH), up(zh, 2, NZH)

    def to_region(target):
        def send(p, carry):
            ty, tc = up(y, lax.rem(p, NY), NY), up(c, p // NY, NC)
            remote(
                picked.at[ty * NC + tc], gathered.at[zh, me], disp_send, disp_recv.at[zh],
                device(y=ty, c=tc, zh=target),
            ).start()
            return carry
        return send

    lax.fori_loop(0, NY * NC, to_region(ahead), 0)
    lax.fori_loop(0, NY * NC, to_region(behind), 0)
    lax.fori_loop(1, NY * NC, to_region(zh), 0)
    pltpu.make_async_copy(picked.at[me], gathered.at[zh, me], disp_recv.at[zh]).start()

    def block(r, bx, by):
        return xbuf.at[r, :, pl.ds(pl.multiple_of(((by * NC + c) * NX + bx) * LANES, LANES), LANES)]

    def spread(r):
        mine = block(r, x, y)
        for s in range(NY * NC):
            for p in range(PAIRS):
                mine[pl.ds((s * PAIRS + p) * 2, 2), :] = gathered[r, s, p]

        def send(p, carry):
            remote(
                mine, mine, ag_send, ag_recv.at[r, p - 1],
                device(x=up(x, lax.rem(p, NX), NX), y=up(y, p // NX, NY)),
            ).start()
            return carry

        lax.fori_loop(1, NX * NY, send, 0)
        remote(mine, mine, fwd_send, fwd_recv.at[r], device(c=1 - c)).start()

    def collect(r):
        def take(p, carry):
            theirs = block(r, up(x, NX - lax.rem(p, NX), NX), up(y, NY - p // NX, NY))
            waits(theirs, ag_recv.at[r, p - 1])
            remote(theirs, theirs, fwd_send, fwd_recv.at[r], device(c=1 - c)).start()
            return carry

        lax.fori_loop(1, NX * NY, take, 0)

    def run(half, ty):
        return pl.ds(pl.multiple_of((ty * NC + half) * NX * LANES, LANES), NX * LANES)

    def compute(r):
        def up_gate(half):
            parts = [
                lax.dot_general(
                    xbuf[r, :, run(half, ty)], wgu[:, run(half, ty)], (((1,), (1,)), ((), ())),
                    preferred_element_type=jnp.float32,
                )
                for ty in range(NY)
            ]
            return (parts[0] + parts[1]) + (parts[2] + parts[3])

        h = up_gate(c)
        with scope("wfwd"):
            waits(xbuf.at[r, :, pl.ds(0, 16 * LANES)], fwd_recv.at[r])
        h = h + up_gate(1 - c)
        g, u = h[:, :128], h[:, 128:]
        act = (g / (1.0 + jnp.exp(-g)) * u).astype(jnp.bfloat16)
        dys = (2, 1, 3, 0)
        for dy in dys:
            ty = up(y, dy, NY)
            ysend[r, ty] = jnp.dot(act, wd[:, run(1 - c, ty)], preferred_element_type=jnp.float32).astype(jnp.bfloat16)
            remote(ysend.at[r, ty], yrecv.at[r, ty], pair_send, pair_recv.at[r, ty], device(c=1 - c)).start()
        for dy in dys:
            ty = up(y, dy, NY)
            both = jnp.dot(act, wd[:, run(c, ty)], preferred_element_type=jnp.float32)
            with scope("wpair"):
                waits(yrecv.at[r, ty], pair_recv.at[r, ty])
            yown[r, ty] = (both + yrecv[r, ty].astype(jnp.float32)).astype(jnp.bfloat16)
            for dx in (2, 1, 3, 0):
                if dx == 0 and dy == 0:
                    continue
                tx = up(x, dx, NX)
                remote(
                    yown.at[r, ty, :, pl.ds(pl.multiple_of(tx * LANES, LANES), LANES)],
                    rrecv.at[r, dy * NX + dx - 1], rs_send, rs_recv.at[r], device(x=tx, y=ty),
                ).start()

    def send_home(r):
        with scope("wrs"):
            waits(rrecv.at[r], rs_recv.at[r])
        acc = yown[r, y, :, pl.ds(pl.multiple_of(x * LANES, LANES), LANES)].astype(jnp.float32)
        for s in range(NX * NY - 1):
            acc = acc + rrecv[r, s].astype(jnp.float32)
        total[...] = acc
        for s in range(NY * NC):
            for p in range(PAIRS):
                homeward[r, s, p] = total[pl.ds((s * PAIRS + p) * 2, 2), :].astype(jnp.bfloat16)

        def send(s, carry):
            ty, tc = s // NC, lax.rem(s, NC)
            dst = arrived.at[zh, zl]
            here = (r == zh) & (ty == y) & (tc == c) & (zl == me)

            @pl.when(here)
            def _():
                pltpu.make_async_copy(homeward.at[r, s], dst, ret_recv).start()

            @pl.when(jnp.logical_not(here))
            def _():
                remote(
                    homeward.at[r, s], dst, ret_send, ret_recv, device(y=ty, c=tc, zh=r, zl=me),
                ).start()
            return carry

        lax.fori_loop(0, NY * NC, send, 0)

    def far_one(k):
        @pl.when(order[k] == across)
        def _():
            waits(gathered.at[order[k]], disp_recv.at[order[k]])

    with scope("wown"):
        waits(gathered.at[zh], disp_recv.at[zh])
    spread(zh)
    with scope("wnear"):
        waits(gathered.at[ahead], disp_recv.at[ahead])
    remote(
        gathered.at[ahead, pl.ds(0, 4)], gathered.at[ahead, pl.ds(0, 4)], disp_send, disp_recv.at[ahead],
        device(zh=behind),
    ).start()
    with scope("wnear"):
        waits(gathered.at[behind], disp_recv.at[behind])
    remote(
        gathered.at[behind, pl.ds(4, 4)], gathered.at[behind, pl.ds(4, 4)], disp_send, disp_recv.at[behind],
        device(zh=ahead),
    ).start()

    @pl.when(order[1] != across)
    def _():
        spread(order[1])

    with scope("col0"):
        collect(zh)
    for load in loads[3:]:
        load.wait()
    with scope("comp0"):
        compute(zh)

    @pl.when(order[1] == across)
    def _():
        with scope("wfar"):
            waits(gathered.at[order[1]], disp_recv.at[order[1]])
        spread(order[1])

    with scope("col1"):
        collect(order[1])
    far_one(2)
    with scope("spread2"):
        spread(order[2])
    with scope("comp1"):
        compute(order[1])
    with scope("col2"):
        collect(order[2])
    far_one(3)
    with scope("spread3"):
        spread(order[3])
    with scope("home0"):
        send_home(zh)
    with scope("comp2"):
        compute(order[2])
    with scope("home1"):
        send_home(order[1])
    with scope("col3"):
        collect(order[3])
    with scope("comp3"):
        compute(order[3])
    with scope("home2"):
        send_home(order[2])
    with scope("home3"):
        send_home(order[3])

    with scope("wret"):
        waits(arrived, ret_recv)
    for e in range(EXPERTS):
        for p in range(PAIRS):
            part = arrived[0, e, p].astype(jnp.float32)
            for k in range(1, NZH):
                part = part + arrived[k, e, p].astype(jnp.float32)
            returned[pl.ds((e * PAIRS + p) * 2, 2), :] = part
    place = lax.broadcasted_iota(jnp.int32, (EXPERTS * SLOTS, tokens), 0)
    gates = gate_ref[...].astype(jnp.float32)
    combining = jnp.where(n_first == place, gates[0:1, :], 0.0) + jnp.where(n_second == place, gates[1:2, :], 0.0)
    mixed = lax.dot_general(
        combining, returned[...], (((0,), (0,)), ((), ())),
        preferred_element_type=jnp.float32, precision=lax.Precision.HIGHEST,
    )
    residual = hid[:, pl.ds(pl.multiple_of((zl * NX + x) * LANES, LANES), LANES)].astype(jnp.float32)
    out_ref[...] = (residual + mixed).astype(jnp.bfloat16)

    with scope("drain"):
        for _ in range(3):
            waits(gathered.at[1], disp_send)
        waits(gathered.at[0, pl.ds(0, 7)], disp_send)
        for r in range(4):
            waits(xbuf.at[r, :, pl.ds(0, 15 * LANES)], ag_send)
            waits(xbuf.at[r, :, pl.ds(0, 16 * LANES)], fwd_send)
            waits(yrecv.at[r], pair_send)
            waits(rrecv.at[r], rs_send)
        waits(arrived.at[pl.ds(0, 3)], ret_send)
        waits(arrived.at[3, pl.ds(0, 7)], ret_send)

        @pl.when(zl != me)
        def _():
            waits(arrived.at[3, 7], ret_send)


def local(hidden_in, expert_ids, gate_vals, w_gate, w_up, w_down):
    tokens, width = hidden_in.shape
    ids = jnp.swapaxes(expert_ids, 0, 1)
    gates = jnp.swapaxes(gate_vals, 0, 1)
    wg = jnp.swapaxes(w_gate[0], 0, 1)
    wu = jnp.swapaxes(w_up[0], 0, 1)
    bf16, f32 = jnp.bfloat16, jnp.float32
    dma, hbm, vmem = pltpu.SemaphoreType.DMA, pl.BlockSpec(memory_space=pltpu.HBM), pl.BlockSpec(memory_space=pltpu.VMEM)
    return pl.pallas_call(
        moe_kernel,
        name="moe",
        out_shape=jax.ShapeDtypeStruct((tokens, LANES), bf16),
        in_specs=[hbm] * 6,
        out_specs=vmem,
        scratch_shapes=[
            pltpu.VMEM((tokens, width), bf16),
            pltpu.VMEM((2, tokens), jnp.int32),
            pltpu.VMEM((2, tokens), bf16),
            pltpu.VMEM((256, width), bf16),
            pltpu.VMEM((128, width), bf16),
            pltpu.VMEM((8, PAIRS, 2, LANES), bf16),
            pltpu.VMEM((4, 8, PAIRS, 2, LANES), bf16),
            pltpu.VMEM((4, ROWS, width), bf16),
            pltpu.VMEM((4, NY, ROWS, NX * LANES), bf16),
            pltpu.VMEM((4, NY, ROWS, NX * LANES), bf16),
            pltpu.VMEM((4, NY, ROWS, NX * LANES), bf16),
            pltpu.VMEM((4, NX * NY - 1, ROWS, LANES), bf16),
            pltpu.VMEM((ROWS, LANES), f32),
            pltpu.VMEM((4, 8, PAIRS, 2, LANES), bf16),
            pltpu.VMEM((4, 8, PAIRS, 2, LANES), bf16),
            pltpu.VMEM((ROWS, LANES), f32),
            dma((6,)), dma, dma((4,)), dma, dma((4, NX * NY - 1)), dma, dma((4,)),
            dma, dma((4, NY)), dma, dma((4,)), dma, dma,
        ],
        compiler_params=pltpu.CompilerParams(
            collective_id=0, has_side_effects=True, vmem_limit_bytes=67043328
        ),
    )(hidden_in, ids, gates, wg, wu, w_down[0])


def solution(mesh):
    split = Mesh(mesh.devices.reshape(NY, NZH, NC, NZL, NX), AXES)
    return jax.shard_map(
        local,
        mesh=split,
        in_specs=(
            P(SEQ, None),
            P(SEQ, None),
            P(SEQ, None),
            P(ET, None, SEQ),
            P(ET, None, SEQ),
            P(ET, SEQ, None),
        ),
        out_specs=P(SEQ, ET),
        check_vma=False,
    )
```

time: 88.3 us -> 78.7 us (0.89)
  the two profiles are of different devices: /device:TPU:24 before, /device:TPU:139 now
where the time goes in v2:
time: 78.7 us; the launch traced here: 78.5 us
  Pallas kernels  77.2 us (98%)
  local copies, waits for them, and re-layouts  1.3 us (2%)
    pallas_call x1, Pallas kernels, local(): pl.pallas_call(moe_kernel, name='moe', out_shape=jax.ShapeDtypeStruct((to...  77.2 us

profile of v2, /device:TPU:139, one launch (start us, length us, event | category | flops | bytes accessed | tf_op | source)
XLA Modules:
  0.0 78.5 jit_solution(16699728844765366882)
XLA Ops:
  0.0 77.2 %moe.1 = bf16[32,128]{1,0:T(8,128)(2,1)} custom-call(bf16[32,4096]{1,0:T(8,128)(2,1)} %hidden_any.1, s32[2,32]{1,0:T(2,128)} %bitcast.12, bf16[2,32]{1,0:T(2,128)(2,1)} %bitcast.13, bf16[112,4096]{1,0:T(8,128)(2,1)} %bitcast.9, bf16[112,4096]{1,0:T(8,128)(2,1)} %bitcast.10, bf16[112,4096]{1,0:T(8,128)(2,1)} %bitcast.11), custom_call_target="tpu_custom_call" | custom-call | tf_op jit(solution)/shard_map/moe/pallas_call | solution.py:352
  77.2 1.3 %copy.8 = bf16[32,128]{1,0:T(8,128)(2,1)} copy(bf16[32,128]{1,0:T(8,128)(2,1)} %moe.1) | data formatting | bytes 16384

commit v3 on v2

v3 whole, which is shorter than its diff:
```python
import functools

import jax
import jax.numpy as jnp
from jax import lax
from jax.experimental import pallas as pl
from jax.experimental.pallas import tpu as pltpu
from jax.sharding import Mesh
from jax.sharding import PartitionSpec as P

EXPERTS = 8
SLOTS = 10
PAIRS = SLOTS // 2
LANES = 128
AXES = ("y", "zh", "c", "zl", "x")
NY, NZH, NC, NZL, NX = 4, 4, 2, 8, 4
SEQ = ("y", "zh", "c")
ET = ("zl", "x")
ROWS = NY * NC * SLOTS
MESH = pl.DeviceIdType.MESH


def moe_kernel(
    hidden_any, ids_any, gate_any, wg_any, wu_any, wd_any,
    out_ref,
    hid, ids_ref, gate_ref, wraw, wup, wdown, picked, gathered, xown, xpair, hidden, ysend, yrecv, yown,
    half, quarter, total, homeward, arrived, returned,
    load_sem, disp_send, disp_recv, ag_send, ag_recv, fwd_send, fwd_recv,
    pair_send, pair_recv, half_send, half_recv, quarter_send, quarter_recv, ret_send, ret_recv,
):
    scope = jax.named_scope
    at = {name: lax.axis_index(name) for name in AXES}
    y, zh, c, zl, x = (at[name] for name in AXES)

    def device(**other):
        return {**at, **other}

    def remote(src, dst, send, recv, dev):
        return pltpu.make_async_remote_copy(
            src_ref=src, dst_ref=dst, send_sem=send, recv_sem=recv, device_id=dev, device_id_type=MESH
        )

    def waits(ref, sem):
        pltpu.make_async_copy(ref, ref, sem).wait()

    def up(v, d, n):
        return lax.rem(v + d, n)

    barrier = pltpu.get_barrier_semaphore()

    def hello(**other):
        pl.semaphore_signal(barrier, inc=1, device_id=device(**other), device_id_type=MESH)

    def hello_plane(p, carry):
        hello(x=up(x, lax.rem(p, NX), NX), y=up(y, p // NX, NY))
        return carry

    def hello_far(p, carry):
        hello(y=up(y, lax.rem(p, NY), NY), c=up(c, p // NY, NC), zh=up(zh, 1, NZH))
        hello(y=up(y, lax.rem(p, NY), NY), c=up(c, p // NY, NC), zh=up(zh, 3, NZH))
        return carry

    def hello_region(p, carry):
        hello(zl=up(zl, p, NZL))
        return carry

    def hello_twin(p, carry):
        hello(y=up(y, p, NY), c=1 - c)
        return carry

    lax.fori_loop(0, NY * NC, hello_far, 0)
    lax.fori_loop(1, NZL, hello_region, 0)
    lax.fori_loop(1, NX * NY, hello_plane, 0)
    lax.fori_loop(0, NY, hello_twin, 0)

    def columns(side, ty):
        core = c if side == 0 else 1 - c
        return pl.ds(pl.multiple_of((ty * NC + core) * NX * LANES, LANES), NX * LANES)

    small = [
        pltpu.make_async_copy(ids_any, ids_ref, load_sem.at[0]),
        pltpu.make_async_copy(gate_any, gate_ref, load_sem.at[1]),
        pltpu.make_async_copy(hidden_any, hid, load_sem.at[2]),
    ]
    loads = []
    for side in range(NC):
        for ty in range(NY):
            to = pl.ds(ty * NX * LANES, NX * LANES)
            loads += [
                pltpu.make_async_copy(wg_any.at[:, columns(side, ty)], wraw.at[side, pl.ds(0, 112), to], load_sem.at[3]),
                pltpu.make_async_copy(wu_any.at[:, columns(side, ty)], wraw.at[side, pl.ds(128, 112), to], load_sem.at[3]),
                pltpu.make_async_copy(wd_any.at[:, columns(side, ty)], wdown.at[side, pl.ds(0, 112), to], load_sem.at[4]),
            ]
    for load in small + loads:
        load.start()
    width = wdown.shape[2]
    for side in range(NC):
        wraw[side, pl.ds(112, 16), :] = jnp.zeros((16, width), jnp.bfloat16)
        wraw[side, pl.ds(240, 16), :] = jnp.zeros((16, width), jnp.bfloat16)
        wdown[side, pl.ds(112, 16), :] = jnp.zeros((16, width), jnp.bfloat16)
    small[0].wait()
    small[1].wait()

    tokens = ids_ref.shape[1]
    ids = ids_ref[...]
    expert = lax.broadcasted_iota(jnp.int32, (EXPERTS, tokens), 0)
    first, second = ids[0:1, :], ids[1:2, :]
    named = (jnp.where(first == expert, 1.0, 0.0) + jnp.where(second == expert, 1.0, 0.0)).astype(jnp.float32)
    before = jnp.where(
        lax.broadcasted_iota(jnp.int32, (tokens, tokens), 0) < lax.broadcasted_iota(jnp.int32, (tokens, tokens), 1),
        1.0, 0.0,
    ).astype(jnp.float32)
    earlier = jnp.dot(named, before, preferred_element_type=jnp.float32)

    def number(chosen):
        slot = jnp.sum(jnp.where(chosen == expert, earlier, 0.0), axis=0, keepdims=True)
        return chosen * SLOTS + slot.astype(jnp.int32)

    n_first, n_second = number(first), number(second)
    wanted = lax.broadcasted_iota(jnp.int32, (16, tokens), 0)
    wanted = jnp.where(wanted < SLOTS, wanted + zl * SLOTS, -1)
    placing = (
        jnp.where(n_first == wanted, 1.0, 0.0) + jnp.where(n_second == wanted, 1.0, 0.0)
    ).astype(jnp.bfloat16)
    small[2].wait()
    for j in range(NZL):
        block = hid[:, pl.ds(pl.multiple_of((j * NX + x) * LANES, LANES), LANES)]
        rows = jnp.dot(placing, block, preferred_element_type=jnp.float32)
        for p in range(PAIRS):
            picked[j, p] = rows[2 * p : 2 * p + 2].astype(jnp.bfloat16)

    me = y * NC + c
    with scope("w_barrier"):
        pl.semaphore_wait(barrier, 2 * NY * NC + (NZL - 1) + (NX * NY - 1) + NY)

    ahead, behind, across = up(zh, 1, NZH), up(zh, 3, NZH), up(zh, 2, NZH)
    odd = lax.rem(zh, 2)
    order = (zh, 1 - odd, 3 - odd, across)

    def to_region(target):
        def send(p, carry):
            ty, tc = up(y, lax.rem(p, NY), NY), up(c, p // NY, NC)
            remote(
                picked.at[ty * NC + tc], gathered.at[zh, me], disp_send, disp_recv.at[zh],
                device(y=ty, c=tc, zh=target),
            ).start()
            return carry
        return send

    lax.fori_loop(0, NY * NC, to_region(ahead), 0)
    lax.fori_loop(0, NY * NC, to_region(behind), 0)
    lax.fori_loop(1, NY * NC, to_region(zh), 0)
    pltpu.make_async_copy(picked.at[me], gathered.at[zh, me], disp_recv.at[zh]).start()

    def shifted(da, db):
        return up(x, da * (1 - c) + db * c, NX), up(y, da * c + db * (1 - c), NY)

    def piece(buf, r, bx, by):
        return buf.at[r, :, pl.ds(pl.multiple_of((by * NX + bx) * LANES, LANES), LANES)]

    def hand_over(r, bx, by):
        remote(piece(xown, r, bx, by), piece(xpair, r, bx, by), fwd_send, fwd_recv.at[r], device(c=1 - c)).start()

    def spread(r):
        mine = piece(xown, r, x, y)
        for s in range(NY * NC):
            for p in range(PAIRS):
                mine[pl.ds((s * PAIRS + p) * 2, 2), :] = gathered[r, s, p]

        def send(d, carry):
            ax, ay = shifted(d, 0)
            remote(mine, mine, ag_send, ag_recv.at[r, d - 1], device(x=ax, y=ay)).start()
            bx, by = shifted(0, d)
            remote(mine, mine, ag_send, ag_recv.at[r, d * NX - 1], device(x=bx, y=by)).start()
            return carry

        lax.fori_loop(1, NX, send, 0)
        hand_over(r, x, y)

    def relay(r):
        def take(da, carry):
            sx, sy = shifted(NX - da, 0)
            theirs = piece(xown, r, sx, sy)
            waits(theirs, ag_recv.at[r, da - 1])

            def send(db, inner):
                bx, by = shifted(0, db)
                remote(theirs, theirs, ag_send, ag_recv.at[r, db * NX + da - 1], device(x=bx, y=by)).start()
                return inner

            lax.fori_loop(1, NY, send, 0)
            hand_over(r, sx, sy)
            return carry

        lax.fori_loop(1, NX, take, 0)

    def collect(r):
        def take(p, carry):
            sx, sy = shifted(lax.rem(NX - lax.rem(p, NX), NX), NY - p // NX)
            waits(piece(xown, r, sx, sy), ag_recv.at[r, p - 1])
            hand_over(r, sx, sy)
            return carry

        lax.fori_loop(NX, NX * NY, take, 0)

    def up_and_down(r):
        h = jnp.dot(xown[r], wup[0], preferred_element_type=jnp.float32)
        with scope("wfwd"):
            waits(xpair.at[r], fwd_recv.at[r])
        h = h + jnp.dot(xpair[r], wup[1], preferred_element_type=jnp.float32)
        g, u = h[:, :128], h[:, 128:]
        act = (g / (1.0 + jnp.exp(-g)) * u).astype(jnp.bfloat16)
        hidden[r] = act
        out = jnp.dot(act, wdown[1], preferred_element_type=jnp.float32).astype(jnp.bfloat16)
        for ty in range(NY):
            for tx in range(NX):
                col = (ty * NX + tx) * LANES
                ysend[r, tx * (1 - c) + ty * c, ty * (1 - c) + tx * c] = out[:, col : col + LANES]
        remote(ysend.at[r], yrecv.at[r], pair_send, pair_recv.at[r], device(c=1 - c)).start()

    mine_b, mine_a = y * (1 - c) + x * c, x * (1 - c) + y * c

    def halve(r):
        out = jnp.dot(hidden[r], wdown[0], preferred_element_type=jnp.float32)
        with scope("wpair"):
            waits(yrecv.at[r], pair_recv.at[r])
        for ty in range(NY):
            for tx in range(NX):
                col = (ty * NX + tx) * LANES
                b, a = ty * (1 - c) + tx * c, tx * (1 - c) + ty * c
                yown[r, b, a] = (out[:, col : col + LANES] + yrecv[r, b, a].astype(jnp.float32)).astype(jnp.bfloat16)

        def send(db, carry):
            bx, by = shifted(0, db)
            remote(
                yown.at[r, up(mine_b, db, NY)], half.at[r, db - 1], half_send, half_recv.at[r], device(x=bx, y=by)
            ).start()
            return carry

        lax.fori_loop(1, NY, send, 0)

    def quarter_sum(r):
        with scope("whalf"):
            waits(half.at[r], half_recv.at[r])
        for a in range(NX):
            acc = yown[r, mine_b, a].astype(jnp.float32)
            for k in range(NY - 1):
                acc = acc + half[r, k, a].astype(jnp.float32)
            yown[r, mine_b, a] = acc.astype(jnp.bfloat16)

        def send(da, carry):
            ax, ay = shifted(da, 0)
            remote(
                yown.at[r, mine_b, up(mine_a, da, NX)], quarter.at[r, da - 1], quarter_send, quarter_recv.at[r],
                device(x=ax, y=ay),
            ).start()
            return carry

        lax.fori_loop(1, NX, send, 0)

    def send_home(r):
        with scope("wquart"):
            waits(quarter.at[r], quarter_recv.at[r])
        acc = yown[r, mine_b, mine_a].astype(jnp.float32)
        for k in range(NX - 1):
            acc = acc + quarter[r, k].astype(jnp.float32)
        total[...] = acc
        for s in range(NY * NC):
            for p in range(PAIRS):
                homeward[r, s, p] = total[pl.ds((s * PAIRS + p) * 2, 2), :].astype(jnp.bfloat16)

        def send(s, carry):
            ty, tc = s // NC, lax.rem(s, NC)
            dst = arrived.at[zh, zl]
            here = (r == zh) & (ty == y) & (tc == c) & (zl == me)

            @pl.when(here)
            def _():
                pltpu.make_async_copy(homeward.at[r, s], dst, ret_recv).start()

            @pl.when(jnp.logical_not(here))
            def _():
                remote(
                    homeward.at[r, s], dst, ret_send, ret_recv, device(y=ty, c=tc, zh=r, zl=me),
                ).start()
            return carry

        lax.fori_loop(0, NY * NC, send, 0)

    own, near_1, near_2, far = order

    with scope("wraw"):
        waits(wraw.at[:, pl.ds(0, 224)], load_sem.at[3])
        waits(wdown.at[:, pl.ds(0, 112)], load_sem.at[4])
    for side in range(NC):
        wup[side] = wraw[side].T
    with scope("wown"):
        waits(gathered.at[own], disp_recv.at[own])
    spread(own)
    with scope("F0"):
        relay(own)
    with scope("wnear"):
        waits(gathered.at[ahead], disp_recv.at[ahead])
    remote(
        gathered.at[ahead, pl.ds(0, 4)], gathered.at[ahead, pl.ds(0, 4)], disp_send, disp_recv.at[ahead],
        device(zh=behind),
    ).start()
    with scope("wnear"):
        waits(gathered.at[behind], disp_recv.at[behind])
    remote(
        gathered.at[behind, pl.ds(4, 4)], gathered.at[behind, pl.ds(4, 4)], disp_send, disp_recv.at[behind],
        device(zh=ahead),
    ).start()
    with scope("S1"):
        spread(near_1)
    with scope("S2"):
        spread(near_2)
    with scope("G0"):
        collect(own)
    with scope("A0"):
        up_and_down(own)
    with scope("F1"):
        relay(near_1)
    with scope("F2"):
        relay(near_2)
    with scope("B0"):
        halve(own)
    with scope("G1"):
        collect(near_1)
    with scope("wfar"):
        waits(gathered.at[far], disp_recv.at[far])
    with scope("S3"):
        spread(far)
    with scope("A1"):
        up_and_down(near_1)
    with scope("Q0"):
        quarter_sum(own)
    with scope("B1"):
        halve(near_1)
    with scope("F3"):
        relay(far)
    with scope("G2"):
        collect(near_2)
    with scope("A2"):
        up_and_down(near_2)
    with scope("Z0"):
        send_home(own)
    with scope("B2"):
        halve(near_2)
    with scope("Q1"):
        quarter_sum(near_1)
    with scope("G3"):
        collect(far)
    with scope("A3"):
        up_and_down(far)
    with scope("Z1"):
        send_home(near_1)
    with scope("Q2"):
        quarter_sum(near_2)
    with scope("B3"):
        halve(far)
    with scope("Z2"):
        send_home(near_2)
    with scope("Q3"):
        quarter_sum(far)
    with scope("Z3"):
        send_home(far)

    with scope("wret"):
        waits(arrived, ret_recv)
    for e in range(EXPERTS):
        for p in range(PAIRS):
            part = arrived[0, e, p].astype(jnp.float32)
            for k in range(1, NZH):
                part = part + arrived[k, e, p].astype(jnp.float32)
            returned[pl.ds((e * PAIRS + p) * 2, 2), :] = part
    place = lax.broadcasted_iota(jnp.int32, (EXPERTS * SLOTS, tokens), 0)
    gates = gate_ref[...].astype(jnp.float32)
    combining = jnp.where(n_first == place, gates[0:1, :], 0.0) + jnp.where(n_second == place, gates[1:2, :], 0.0)
    mixed = lax.dot_general(
        combining, returned[...], (((0,), (0,)), ((), ())),
        preferred_element_type=jnp.float32, precision=lax.Precision.HIGHEST,
    )
    residual = hid[:, pl.ds(pl.multiple_of((zl * NX + x) * LANES, LANES), LANES)].astype(jnp.float32)
    out_ref[...] = (residual + mixed).astype(jnp.bfloat16)

    with scope("drain"):
        for _ in range(3):
            waits(gathered.at[1], disp_send)
        waits(gathered.at[0, pl.ds(0, 7)], disp_send)
        for r in range(4):
            waits(xown.at[r, :, pl.ds(0, 15 * LANES)], ag_send)
            waits(xown.at[r], fwd_send)
            waits(yrecv.at[r], pair_send)
            waits(half.at[r], half_send)
            waits(quarter.at[r], quarter_send)
        waits(arrived.at[pl.ds(0, 3)], ret_send)
        waits(arrived.at[3, pl.ds(0, 7)], ret_send)

        @pl.when(zl != me)
        def _():
            waits(arrived.at[3, 7], ret_send)


def local(hidden_in, expert_ids, gate_vals, w_gate, w_up, w_down):
    tokens, width = hidden_in.shape
    ids = jnp.swapaxes(expert_ids, 0, 1)
    gates = jnp.swapaxes(gate_vals, 0, 1)
    wg = jnp.swapaxes(w_gate[0], 0, 1)
    wu = jnp.swapaxes(w_up[0], 0, 1)
    bf16, f32 = jnp.bfloat16, jnp.float32
    dma, hbm, vmem = pltpu.SemaphoreType.DMA, pl.BlockSpec(memory_space=pltpu.HBM), pl.BlockSpec(memory_space=pltpu.VMEM)
    return pl.pallas_call(
        moe_kernel,
        name="moe",
        out_shape=jax.ShapeDtypeStruct((tokens, LANES), bf16),
        in_specs=[hbm] * 6,
        out_specs=vmem,
        scratch_shapes=[
            pltpu.VMEM((tokens, width), bf16),
            pltpu.VMEM((2, tokens), jnp.int32),
            pltpu.VMEM((2, tokens), bf16),
            pltpu.VMEM((2, 256, width // 2), bf16),
            pltpu.VMEM((2, width // 2, 256), bf16),
            pltpu.VMEM((2, 128, width // 2), bf16),
            pltpu.VMEM((8, PAIRS, 2, LANES), bf16),
            pltpu.VMEM((4, 8, PAIRS, 2, LANES), bf16),
            pltpu.VMEM((4, ROWS, width // 2), bf16),
            pltpu.VMEM((4, ROWS, width // 2), bf16),
            pltpu.VMEM((4, ROWS, LANES), bf16),
            pltpu.VMEM((4, NY, NX, ROWS, LANES), bf16),
            pltpu.VMEM((4, NY, NX, ROWS, LANES), bf16),
            pltpu.VMEM((4, NY, NX, ROWS, LANES), bf16),
            pltpu.VMEM((4, NY - 1, NX, ROWS, LANES), bf16),
            pltpu.VMEM((4, NX - 1, ROWS, LANES), bf16),
            pltpu.VMEM((ROWS, LANES), f32),
            pltpu.VMEM((4, 8, PAIRS, 2, LANES), bf16),
            pltpu.VMEM((4, 8, PAIRS, 2, LANES), bf16),
            pltpu.VMEM((ROWS, LANES), f32),
            dma((5,)), dma, dma((4,)), dma, dma((4, NX * NY - 1)), dma, dma((4,)),
            dma, dma((4,)), dma, dma((4,)), dma, dma((4,)), dma, dma,
        ],
        compiler_params=pltpu.CompilerParams(
            collective_id=0, has_side_effects=True, vmem_limit_bytes=48 * 1024 * 1024
        ),
    )(*(pltpu.with_memory_space_constraint(a, pltpu.HBM) for a in (hidden_in, ids, gates, wg, wu, w_down[0])))


def solution(mesh):
    split = Mesh(mesh.devices.reshape(NY, NZH, NC, NZL, NX), AXES)
    return jax.shard_map(
        local,
        mesh=split,
        in_specs=(
            P(SEQ, None),
            P(SEQ, None),
            P(SEQ, None),
            P(ET, None, SEQ),
            P(ET, None, SEQ),
            P(ET, SEQ, None),
        ),
        out_specs=P(SEQ, ET),
        check_vma=False,
    )
```

time: 78.7 us -> 84.1 us (1.069)
  the two profiles are of different devices: /device:TPU:139 before, /device:TPU:24 now
where the time goes in v3:
time: 84.1 us; the launch traced here: 83.7 us
  Pallas kernels  83.1 us (99%)
    pallas_call x1, Pallas kernels, local(): pl.pallas_call(moe_kernel, name='moe', out_shape=jax.ShapeDtypeStruct((to...  83.1 us

profile of v3, /device:TPU:24, one launch (start us, length us, event | category | flops | bytes accessed | tf_op | source)
XLA Modules:
  0.0 83.7 jit_solution(13284208641204808020)
XLA Ops:
  0.0 83.1 %moe.1 = bf16[32,128]{1,0:T(8,128)(2,1)S(1)} custom-call(bf16[32,4096]{1,0:T(8,128)(2,1)} %hidden_any.1, s32[2,32]{1,0:T(2,128)} %bitcast.12, bf16[2,32]{1,0:T(2,128)(2,1)} %bitcast.13, bf16[112,4096]{1,0:T(8,128)(2,1)} %bitcast.9, bf16[112,4096]{1,0:T(8,128)(2,1)} %bitcast.10, bf16[112,4096]{1,0:T(8,128)(2,1)} %bitcast.11), custom_call_target="tpu_custom_call" | custom-call | tf_op jit(solution)/shard_map/moe/pallas_call | solution.py:413
  83.1 0.6 copy.8

commit v4 on v0

v4 whole, which is shorter than its diff:
```python
import jax
import jax.numpy as jnp
from jax import lax
from jax.experimental import pallas as pl
from jax.experimental.pallas import tpu as pltpu
from jax.sharding import Mesh
from jax.sharding import PartitionSpec as P

EXPERTS = 8
SLOTS = 10
PAIRS = SLOTS // 2
LANES = 128
AXES = ("y", "zh", "c", "zl", "x")
NY, NZH, NC, NZL, NX = 4, 4, 2, 8, 4
SEQ = ("y", "zh", "c")
ET = ("zl", "x")
ROWS = NY * SLOTS
UNITS = 112
PLANE = NX * NY
MESH = pl.DeviceIdType.MESH


def moe_kernel(
    hidden_any, ids_any, gate_any, wg_any, wu_any, wd_any,
    out_ref,
    hid, ids_ref, gate_ref, wraw, wup, wdown, picked, passed, gathered, xbuf, ybuf, summed, total, homeward, arrived, returned,
    load_sem, twin_send, twin_recv, leg_recv, disp_send, disp_recv, ag_send, ag_recv, rs_send, rs_recv, ret_send, ret_recv,
):
    scope = jax.named_scope
    at = {name: lax.axis_index(name) for name in AXES}
    y, zh, c, zl, x = (at[name] for name in AXES)

    def device(**other):
        return {**at, **other}

    def remote(src, dst, send, recv, dev):
        return pltpu.make_async_remote_copy(
            src_ref=src, dst_ref=dst, send_sem=send, recv_sem=recv, device_id=dev, device_id_type=MESH
        )

    def waits(ref, sem):
        pltpu.make_async_copy(ref, ref, sem).wait()

    def up(v, d, n):
        return lax.rem(v + d, n)

    ahead, behind, across = up(zh, 1, NZH), up(zh, 3, NZH), up(zh, 2, NZH)

    barrier = pltpu.get_barrier_semaphore()

    def hello(**other):
        pl.semaphore_signal(barrier, inc=1, device_id=device(**other), device_id_type=MESH)

    def hello_near(d, carry):
        hello(y=up(y, d, NY), zh=ahead)
        hello(y=up(y, d, NY), zh=behind)
        return carry

    high, relays = zl >= NZL // 2, (zl >= 2) & (zl < 6)

    def along(step):
        z = lax.rem(zh * NZL + zl + step + NZH * NZL, NZH * NZL)
        return {"zh": z // NZL, "zl": lax.rem(z, NZL)}

    def hello_relay(d, carry):
        hello(y=up(y, d, NY), **along(jnp.where(high, 6, -6)))
        return carry

    def hello_line(d, carry):
        hello(zl=up(zl, d, NZL))
        return carry

    def hello_plane(p, carry):
        hello(x=up(x, lax.rem(p, NX), NX), y=up(y, p // NX, NY))
        return carry

    lax.fori_loop(0, NY, hello_near, 0)
    lax.fori_loop(0, NY, hello_relay, 0)

    @pl.when(relays)
    def _():
        hello(**along(6))
        hello(**along(-6))

    lax.fori_loop(1, NZL, hello_line, 0)
    lax.fori_loop(1, PLANE, hello_plane, 0)
    hello(c=1 - c)

    width = wdown.shape[2]
    small = [
        pltpu.make_async_copy(ids_any, ids_ref, load_sem.at[0]),
        pltpu.make_async_copy(gate_any, gate_ref, load_sem.at[1]),
        pltpu.make_async_copy(hidden_any, hid, load_sem.at[2]),
    ]
    parts = []
    for h in range(2):
        for ty in range(NY):
            cols, to = pl.ds((2 * ty + h) * NX * LANES, NX * LANES), pl.ds(ty * NX * LANES, NX * LANES)
            for k, (weight, buf, own, twin) in enumerate(
                ((wg_any, wraw, 0, 256), (wu_any, wraw, 128, 384), (wd_any, wdown, 0, 128))
            ):
                parts.append((
                    weight.at[:, cols], buf.at[h, pl.ds(own, UNITS), to], buf.at[h, pl.ds(twin, UNITS), to], 3 + k // 2
                ))
    loads = [pltpu.make_async_copy(part, own, load_sem.at[sem]) for part, own, _, sem in parts]
    for load in small + loads:
        load.start()
    blank = jnp.zeros((128 - UNITS, width), jnp.bfloat16)
    for h in range(2):
        for k in range(4):
            wraw[h, pl.ds(k * 128 + UNITS, 128 - UNITS), :] = blank
        for k in range(2):
            wdown[h, pl.ds(k * 128 + UNITS, 128 - UNITS), :] = blank
    small[0].wait()
    small[1].wait()

    tokens = ids_ref.shape[1]
    ids = ids_ref[...]
    expert = lax.broadcasted_iota(jnp.int32, (EXPERTS, tokens), 0)
    first, second = ids[0:1, :], ids[1:2, :]
    named = (jnp.where(first == expert, 1.0, 0.0) + jnp.where(second == expert, 1.0, 0.0)).astype(jnp.float32)
    before = jnp.where(
        lax.broadcasted_iota(jnp.int32, (tokens, tokens), 0) < lax.broadcasted_iota(jnp.int32, (tokens, tokens), 1),
        1.0, 0.0,
    ).astype(jnp.float32)
    earlier = jnp.dot(named, before, preferred_element_type=jnp.float32)

    def number(chosen):
        slot = jnp.sum(jnp.where(chosen == expert, earlier, 0.0), axis=0, keepdims=True)
        return chosen * SLOTS + slot.astype(jnp.int32)

    n_first, n_second = number(first), number(second)
    slot = lax.broadcasted_iota(jnp.int32, (16, tokens), 0)

    def placing(expert_here):
        wanted = jnp.where(slot < SLOTS, slot + expert_here * SLOTS, -1)
        return (
            jnp.where(n_first == wanted, 1.0, 0.0) + jnp.where(n_second == wanted, 1.0, 0.0)
        ).astype(jnp.bfloat16)

    places = jnp.concatenate([placing(zl), placing(lax.rem(zl + NZL // 2, NZL))], axis=0)
    small[2].wait()
    for j in range(NZL):
        block = hid[:, pl.ds(pl.multiple_of((j * NX + x) * LANES, LANES), LANES)]
        rows = jnp.dot(places, block, preferred_element_type=jnp.float32)
        for k in range(2):
            for p in range(PAIRS):
                picked[k, j // 2, j % 2, p] = rows[16 * k + 2 * p : 16 * k + 2 * p + 2].astype(jnp.bfloat16)

    with scope("w_barrier"):
        pl.semaphore_wait(barrier, 2 * NY + (NZL - 1) + (PLANE - 1) + 2 + jnp.where(relays, 2 * NY, 0))

    order = (
        jnp.where(zh == 0, 0, jnp.where(zh == 1, 1, jnp.where(zh == 2, 2, 3))),
        jnp.where(zh == 0, 1, jnp.where(zh == 1, 0, jnp.where(zh == 2, 1, 0))),
        jnp.where(zh == 0, 3, jnp.where(zh == 1, 2, jnp.where(zh == 2, 0, 2))),
        jnp.where(zh == 0, 2, jnp.where(zh == 1, 3, jnp.where(zh == 2, 3, 1))),
    )
    work = (
        jnp.where(zh == 0, 0, jnp.where(zh == 1, 1, jnp.where(zh == 2, 0, 3))),
        jnp.where(zh == 0, 1, jnp.where(zh == 1, 0, jnp.where(zh == 2, 1, 0))),
        jnp.where(zh == 0, 3, jnp.where(zh == 1, 2, jnp.where(zh == 2, 2, 2))),
        jnp.where(zh == 0, 2, jnp.where(zh == 1, 3, jnp.where(zh == 2, 3, 1))),
    )

    @pl.when(high)
    def _():
        remote(picked.at[1], passed.at[0], disp_send, leg_recv.at[0], device(**along(6))).start()

    @pl.when(jnp.logical_not(high))
    def _():
        remote(picked.at[1], passed.at[1], disp_send, leg_recv.at[1], device(**along(-6))).start()

    def to_region(target):
        def send(d, carry):
            ty = up(y, d, NY)
            remote(
                picked.at[0, ty], gathered.at[zh, y], disp_send, disp_recv.at[zh], device(y=ty, zh=target)
            ).start()
            return carry
        return send

    @pl.when(c == 0)
    def _():
        lax.fori_loop(0, NY, to_region(jnp.where(high, ahead, behind)), 0)

    lax.fori_loop(1, NY, to_region(zh), 0)
    pltpu.make_async_copy(picked.at[0, y], gathered.at[zh, y], disp_recv.at[zh]).start()

    def second_leg(way, source, step):
        waits(passed.at[way], leg_recv.at[way])

        def send(d, carry):
            ty = up(y, d, NY)
            remote(
                passed.at[way, ty], gathered.at[source, y], disp_send, disp_recv.at[source], device(y=ty, **along(step))
            ).start()
            return carry

        lax.fori_loop(0, NY, send, 0)

    def piece(r, tx, ty):
        return xbuf.at[r, :, :, pl.ds(pl.multiple_of((ty * NX + tx) * LANES, LANES), LANES)]

    def spread(r):
        mine = piece(r, x, y)
        for s in range(NY):
            for h in range(2):
                for p in range(PAIRS):
                    mine[h, pl.ds((s * PAIRS + p) * 2, 2), :] = gathered[r, s, h, p]

        def send(p, carry):
            remote(
                mine, mine, ag_send, ag_recv.at[r], device(x=up(x, lax.rem(p, NX), NX), y=up(y, p // NX, NY))
            ).start()
            return carry

        lax.fori_loop(1, PLANE, send, 0)

    def compute(r):
        with scope("wag"):
            waits(xbuf.at[r, :, :, pl.ds(0, (PLANE - 1) * LANES)], ag_recv.at[r])
        up_gate = jnp.dot(xbuf[r, 0], wup[0], preferred_element_type=jnp.float32)
        up_gate = up_gate + jnp.dot(xbuf[r, 1], wup[1], preferred_element_type=jnp.float32)

        def swish(k):
            g, u = up_gate[:, k * 256 : k * 256 + 128], up_gate[:, k * 256 + 128 : k * 256 + 256]
            return (g / (1.0 + jnp.exp(-g)) * u).astype(jnp.bfloat16)

        act = jnp.concatenate([swish(0), swish(1)], axis=1)
        for dy in (2, 1, 3, 0):
            ty = up(y, dy, NY)
            cols = pl.ds(pl.multiple_of(ty * NX * LANES, NX * LANES), NX * LANES)
            for h in range(2):
                out = jnp.dot(act, wdown[h, :, cols], preferred_element_type=jnp.float32).astype(jnp.bfloat16)
                for tx in range(NX):
                    ybuf[r, ty, tx, h] = out[:, tx * LANES : (tx + 1) * LANES]
            for dx in (2, 1, 3, 0):
                if dx == 0 and dy == 0:
                    continue
                tx = up(x, dx, NX)
                remote(
                    ybuf.at[r, ty, tx], summed.at[r, dy * NX + dx - 1], rs_send, rs_recv.at[r], device(x=tx, y=ty)
                ).start()

    def send_home(r):
        with scope("wrs"):
            waits(summed.at[r], rs_recv.at[r])
        acc = ybuf[r, y, x].astype(jnp.float32)
        for s in range(PLANE - 1):
            acc = acc + summed[r, s].astype(jnp.float32)
        total[...] = acc
        for s in range(NY):
            for h in range(2):
                for p in range(PAIRS):
                    homeward[r, s, h, p] = total[h, pl.ds((s * PAIRS + p) * 2, 2), :].astype(jnp.bfloat16)

        def send(k, carry):
            ty, h = k // 2, lax.rem(k, 2)
            tz = 2 * y + h
            dst = arrived.at[zh, zl]
            here = (r == zh) & (ty == y) & (tz == zl)

            @pl.when(here)
            def _():
                pltpu.make_async_copy(homeward.at[r, ty, h], dst, ret_recv).start()

            @pl.when(jnp.logical_not(here))
            def _():
                remote(homeward.at[r, ty, h], dst, ret_send, ret_recv, device(y=ty, zh=r, zl=tz)).start()
            return carry

        lax.fori_loop(0, 2 * NY, send, 0)

    with scope("wraw"):
        waits(wraw.at[:, pl.ds(0, 2 * UNITS)], load_sem.at[3])
        waits(wdown.at[:, pl.ds(0, UNITS)], load_sem.at[4])
    for h in range(2):
        wup[h, :, pl.ds(0, 256)] = wraw[h, pl.ds(0, 256), :].T

    @pl.when(c == 0)
    def _():
        lax.fori_loop(0, NY, to_region(jnp.where(high, behind, ahead)), 0)

    with scope("wS0"):
        waits(gathered.at[order[0]], disp_recv.at[order[0]])
    with scope("S0"):
        spread(order[0])
    @pl.when(c == 1)
    def _():
        lax.fori_loop(0, NY, to_region(ahead), 0)
        lax.fori_loop(0, NY, to_region(behind), 0)

    with scope("R"):
        @pl.when(relays & (zh == 3))
        def _():
            second_leg(1, ahead, -6)

        @pl.when(relays)
        def _():
            second_leg(0, behind, 6)

        @pl.when(relays & (zh != 3))
        def _():
            second_leg(1, ahead, -6)

    for part, _, twin, _ in parts:
        remote(part, twin, twin_send, twin_recv, device(c=1 - c)).start()
    with scope("wS1"):
        waits(gathered.at[order[1]], disp_recv.at[order[1]])
    with scope("S1"):
        spread(order[1])
    with scope("wtwin"):
        waits(wraw.at[:, pl.ds(0, 3 * UNITS)], twin_recv)
    for h in range(2):
        wup[h, :, pl.ds(256, 256)] = wraw[h, pl.ds(256, 256), :].T
    with scope("wS2"):
        waits(gathered.at[order[2]], disp_recv.at[order[2]])
    with scope("S2"):
        spread(order[2])
    @pl.when(zh == 0)
    def _():
        with scope("A0"):
            compute(work[0])
        with scope("wS3"):
            waits(gathered.at[order[3]], disp_recv.at[order[3]])
        with scope("S3"):
            spread(order[3])
        with scope("A1"):
            compute(work[1])
        with scope("A2"):
            compute(work[2])
        with scope("Z0"):
            send_home(work[0])
        with scope("A3"):
            compute(work[3])
        with scope("Z1"):
            send_home(work[1])
        with scope("Z2"):
            send_home(work[2])
        with scope("Z3"):
            send_home(work[3])

    @pl.when(zh != 0)
    def _():
        with scope("A0"):
            compute(work[0])
        with scope("wS3"):
            waits(gathered.at[order[3]], disp_recv.at[order[3]])
        with scope("S3"):
            spread(order[3])
        with scope("A1"):
            compute(work[1])
        with scope("Z0"):
            send_home(work[0])
        with scope("A2"):
            compute(work[2])
        with scope("Z1"):
            send_home(work[1])
        with scope("A3"):
            compute(work[3])
        with scope("Z2"):
            send_home(work[2])
        with scope("Z3"):
            send_home(work[3])

    with scope("wret"):
        waits(arrived, ret_recv)
    for e in range(EXPERTS):
        for p in range(PAIRS):
            part = arrived[0, e, p].astype(jnp.float32)
            for k in range(1, NZH):
                part = part + arrived[k, e, p].astype(jnp.float32)
            returned[pl.ds((e * PAIRS + p) * 2, 2), :] = part
    place = lax.broadcasted_iota(jnp.int32, (EXPERTS * SLOTS, tokens), 0)
    gates = gate_ref[...].astype(jnp.float32)
    combining = jnp.where(n_first == place, gates[0:1, :], 0.0) + jnp.where(n_second == place, gates[1:2, :], 0.0)
    mixed = lax.dot_general(
        combining, returned[...], (((0,), (0,)), ((), ())),
        preferred_element_type=jnp.float32, precision=lax.Precision.HIGHEST,
    )
    residual = hid[:, pl.ds(pl.multiple_of((zl * NX + x) * LANES, LANES), LANES)].astype(jnp.float32)
    out_ref[...] = (residual + mixed).astype(jnp.bfloat16)

    with scope("drain"):
        waits(wraw.at[:, pl.ds(0, 3 * UNITS)], twin_send)
        for _ in range(3):
            waits(gathered.at[1], disp_send)
        waits(gathered.at[0, pl.ds(0, 3)], disp_send)

        @pl.when(relays)
        def _():
            waits(gathered.at[pl.ds(0, 2)], disp_send)

        for r in range(NZH):
            waits(xbuf.at[r, :, :, pl.ds(0, (PLANE - 1) * LANES)], ag_send)
            waits(summed.at[r], rs_send)
        waits(arrived.at[pl.ds(0, 3)], ret_send)
        waits(arrived.at[3, pl.ds(0, 7)], ret_send)

        @pl.when((zl != 2 * y) & (zl != 2 * y + 1))
        def _():
            waits(arrived.at[3, 7], ret_send)


def local(hidden_in, expert_ids, gate_vals, w_gate, w_up, w_down):
    tokens, width = hidden_in.shape
    ids = jnp.swapaxes(expert_ids, 0, 1)
    gates = jnp.swapaxes(gate_vals, 0, 1)
    wg = jnp.swapaxes(w_gate[0], 0, 1)
    wu = jnp.swapaxes(w_up[0], 0, 1)
    bf16, f32 = jnp.bfloat16, jnp.float32
    dma, hbm, vmem = pltpu.SemaphoreType.DMA, pl.BlockSpec(memory_space=pltpu.HBM), pl.BlockSpec(memory_space=pltpu.VMEM)
    return pl.pallas_call(
        moe_kernel,
        name="moe",
        out_shape=jax.ShapeDtypeStruct((tokens, LANES), bf16),
        in_specs=[hbm] * 6,
        out_specs=vmem,
        scratch_shapes=[
            pltpu.VMEM((tokens, width), bf16),
            pltpu.VMEM((2, tokens), jnp.int32),
            pltpu.VMEM((2, tokens), bf16),
            pltpu.VMEM((2, 512, width // 2), bf16),
            pltpu.VMEM((2, width // 2, 512), bf16),
            pltpu.VMEM((2, 256, width // 2), bf16),
            pltpu.VMEM((2, NY, 2, PAIRS, 2, LANES), bf16),
            pltpu.VMEM((2, NY, 2, PAIRS, 2, LANES), bf16),
            pltpu.VMEM((NZH, NY, 2, PAIRS, 2, LANES), bf16),
            pltpu.VMEM((NZH, 2, ROWS, width // 2), bf16),
            pltpu.VMEM((NZH, NY, NX, 2, ROWS, LANES), bf16),
            pltpu.VMEM((NZH, PLANE - 1, 2, ROWS, LANES), bf16),
            pltpu.VMEM((2, ROWS, LANES), f32),
            pltpu.VMEM((NZH, NY, 2, PAIRS, 2, LANES), bf16),
            pltpu.VMEM((NZH, NZL, PAIRS, 2, LANES), bf16),
            pltpu.VMEM((EXPERTS * SLOTS, LANES), f32),
            dma((5,)), dma, dma, dma((2,)), dma, dma((4,)), dma, dma((4,)), dma, dma((4,)), dma, dma,
        ],
        compiler_params=pltpu.CompilerParams(
            collective_id=0, has_side_effects=True, vmem_limit_bytes=48 * 1024 * 1024
        ),
    )(*(pltpu.with_memory_space_constraint(a, pltpu.HBM) for a in (hidden_in, ids, gates, wg, wu, w_down[0])))


def solution(mesh):
    split = Mesh(mesh.devices.reshape(NY, NZH, NC, NZL, NX), AXES)
    return jax.shard_map(
        local,
        mesh=split,
        in_specs=(
            P(SEQ, None),
            P(SEQ, None),
            P(SEQ, None),
            P(ET, None, SEQ),
            P(ET, None, SEQ),
            P(ET, SEQ, None),
        ),
        out_specs=P(SEQ, ET),
        check_vma=False,
    )
```

time: 497 us -> 71.2 us (0.14)
  waiting for transfers between devices: 438 us -> 0 us
  Pallas kernels: 0 us -> 69.3 us
  local copies, waits for them, and re-layouts: 18.4 us -> 0.6 us
  between operations: 13.2 us -> 0.01 us
  starting transfers between devices: 12 us -> 0 us
  matrix products: 11.4 us -> 0 us
    reduce_scatter x2 -> x0, waiting for transfers between devices: 239 us -> none  [the longest x1 220 us: scatter_pairs(): return lax.psum_scatter(pieces, chips, scatter_dimension=0, tiled=True)[0]]
    all_gather x1 -> x0, waiting for transfers between devices: 182 us -> none  [local(): segment = lax.all_gather(buffer, SEQ, axis=0, tiled=True)]
    pallas_call x0 -> x1, Pallas kernels: none -> 69.3 us  [local(): pl.pallas_call(moe_kernel, name='moe', out_shape=jax.ShapeDtypeStruct((to...]
    all_to_all x1 -> x0, waiting for transfers between devices: 16.8 us -> none  [sum_at_owner(): pieces = lax.all_to_all(split_up(array, dim, count), axis, 0, 0, tiled=True)]
    all_to_all x1 -> x0, starting transfers between devices: 11.9 us -> none  [sum_at_owner(): pieces = lax.all_to_all(split_up(array, dim, count), axis, 0, 0, tiled=True)]
    dot_general x4 -> x0, matrix products: 11.4 us -> none  [the longest x1 5.62 us: local(): jnp.dot(activations, down_local, preferred_element_type=jnp.float32)]
    transpose x1 -> x0, local copies, waits for them, and re-layouts: 5.15 us -> none  [scatter_pairs(): pieces = pieces.reshape(*sizes, *inside).swapaxes(0, 1).reshape(-1, *inside)]
  transfers between devices with their start and end apart: 4 -> 0, of which waited for: 4 -> 0; matrix products, arithmetic and copies ran while one was open for 0% -> 0% of each run, Pallas kernels for 0% -> 0%
where the time goes in v4:
time: 71.2 us; the launch traced here: 69.9 us
  Pallas kernels  69.3 us (97%)
    pallas_call x1, Pallas kernels, local(): pl.pallas_call(moe_kernel, name='moe', out_shape=jax.ShapeDtypeStruct((to...  69.3 us

profile of v4, /device:TPU:24, one launch (start us, length us, event | category | flops | bytes accessed | tf_op | source)
XLA Modules:
  0.0 69.9 jit_solution(9733029570289110588)
XLA Ops:
  0.0 69.3 %moe.1 = bf16[32,128]{1,0:T(8,128)(2,1)S(1)} custom-call(bf16[32,4096]{1,0:T(8,128)(2,1)} %hidden_any.1, s32[2,32]{1,0:T(2,128)} %bitcast.12, bf16[2,32]{1,0:T(2,128)(2,1)} %bitcast.13, bf16[112,4096]{1,0:T(8,128)(2,1)} %bitcast.9, bf16[112,4096]{1,0:T(8,128)(2,1)} %bitcast.10, bf16[112,4096]{1,0:T(8,128)(2,1)} %bitcast.11), custom_call_target="tpu_custom_call" | custom-call | tf_op jit(solution)/shard_map/moe/pallas_call | solution.py:414
  69.3 0.6 copy.8

commit v5 on v4

--- a/solution.py
+++ b/solution.py
@@ -23,8 +23,9 @@
 def moe_kernel(
     hidden_any, ids_any, gate_any, wg_any, wu_any, wd_any,
     out_ref,
-    hid, ids_ref, gate_ref, wraw, wup, wdown, picked, passed, gathered, xbuf, ybuf, summed, total, homeward, arrived, returned,
-    load_sem, twin_send, twin_recv, leg_recv, disp_send, disp_recv, ag_send, ag_recv, rs_send, rs_recv, ret_send, ret_recv,
+    hid, ids_ref, gate_ref, wraw, wup, wdown, picked, passed, gathered, xbuf, ybuf, half, quarter, whole, total, homeward, arrived, returned,
+    load_sem, twin_send, twin_recv, leg_recv, disp_send, disp_recv, ag_send, ag_recv,
+    half_send, half_recv, quarter_send, quarter_recv, whole_send, whole_recv, ret_send, ret_recv,
 ):
     scope = jax.named_scope
     at = {name: lax.axis_index(name) for name in AXES}
@@ -153,14 +154,14 @@
     order = (
         jnp.where(zh == 0, 0, jnp.where(zh == 1, 1, jnp.where(zh == 2, 2, 3))),
         jnp.where(zh == 0, 1, jnp.where(zh == 1, 0, jnp.where(zh == 2, 1, 0))),
-        jnp.where(zh == 0, 3, jnp.where(zh == 1, 2, jnp.where(zh == 2, 0, 2))),
-        jnp.where(zh == 0, 2, jnp.where(zh == 1, 3, jnp.where(zh == 2, 3, 1))),
+        jnp.where(zh == 0, 3, jnp.where(zh == 1, 2, jnp.where(zh == 2, 0, 1))),
+        jnp.where(zh == 0, 2, jnp.where(zh == 1, 3, jnp.where(zh == 2, 3, 2))),
     )
     work = (
         jnp.where(zh == 0, 0, jnp.where(zh == 1, 1, jnp.where(zh == 2, 0, 3))),
         jnp.where(zh == 0, 1, jnp.where(zh == 1, 0, jnp.where(zh == 2, 1, 0))),
-        jnp.where(zh == 0, 3, jnp.where(zh == 1, 2, jnp.where(zh == 2, 2, 2))),
-        jnp.where(zh == 0, 2, jnp.where(zh == 1, 3, jnp.where(zh == 2, 3, 1))),
+        jnp.where(zh == 0, 3, jnp.where(zh == 1, 2, jnp.where(zh == 2, 2, 1))),
+        jnp.where(zh == 0, 2, jnp.where(zh == 1, 3, jnp.where(zh == 2, 3, 2))),
     )
 
     @pl.when(high)
@@ -199,27 +200,57 @@
 
         lax.fori_loop(0, NY, send, 0)
 
+    def shifted(da, db):
+        return up(x, da * (1 - c) + db * c, NX), up(y, da * c + db * (1 - c), NY)
+
+    def where_to(tx, ty):
+        return ty * (1 - c) + tx * c, tx * (1 - c) + ty * c
+
+    my_b, my_a = where_to(x, y)
+
     def piece(r, tx, ty):
         return xbuf.at[r, :, :, pl.ds(pl.multiple_of((ty * NX + tx) * LANES, LANES), LANES)]
 
-    def spread(r):
+    def share(r, tx, ty, da, db, step):
+        px, py = shifted(da, db)
+        remote(piece(r, tx, ty), piece(r, tx, ty), ag_send, ag_recv.at[r, step], device(x=px, y=py)).start()
+
+    def spread(r, direct):
         mine = piece(r, x, y)
         for s in range(NY):
             for h in range(2):
                 for p in range(PAIRS):
                     mine[h, pl.ds((s * PAIRS + p) * 2, 2), :] = gathered[r, s, h, p]
 
-        def send(p, carry):
-            remote(
-                mine, mine, ag_send, ag_recv.at[r], device(x=up(x, lax.rem(p, NX), NX), y=up(y, p // NX, NY))
-            ).start()
+        def send_all(p, carry):
+            share(r, x, y, lax.rem(p, NX), p // NX, 1)
             return carry
 
-        lax.fori_loop(1, PLANE, send, 0)
-
-    def compute(r):
+        def send_axes(d, carry):
+            share(r, x, y, d, 0, 0)
+            share(r, x, y, 0, d, 1)
+            return carry
+
+        if direct:
+            lax.fori_loop(1, PLANE, send_all, 0)
+        else:
+            lax.fori_loop(1, NX, send_axes, 0)
+
+    def pass_on(r):
+        with scope("wrow"):
+            waits(xbuf.at[r, :, :, pl.ds(0, (NX - 1) * LANES)], ag_recv.at[r, 0])
+
+        def take(da, carry):
+            tx, ty = shifted(da, 0)
+            for db in range(1, NY):
+                share(r, tx, ty, 0, db, 1)
+            return carry
+
+        lax.fori_loop(1, NX, take, 0)
+
+    def compute(r, direct, direct_sum):
         with scope("wag"):
-            waits(xbuf.at[r, :, :, pl.ds(0, (PLANE - 1) * LANES)], ag_recv.at[r])
+            waits(xbuf.at[r, :, :, pl.ds(0, (PLANE - 1 if direct else PLANE - NX) * LANES)], ag_recv.at[r, 1])
         up_gate = jnp.dot(xbuf[r, 0], wup[0], preferred_element_type=jnp.float32)
         up_gate = up_gate + jnp.dot(xbuf[r, 1], wup[1], preferred_element_type=jnp.float32)
 
@@ -234,21 +265,52 @@
             for h in range(2):
                 out = jnp.dot(act, wdown[h, :, cols], preferred_element_type=jnp.float32).astype(jnp.bfloat16)
                 for tx in range(NX):
-                    ybuf[r, ty, tx, h] = out[:, tx * LANES : (tx + 1) * LANES]
+                    to_b, to_a = where_to(tx, ty)
+                    ybuf[r, to_b, to_a, h] = out[:, tx * LANES : (tx + 1) * LANES]
+            if not direct_sum:
+                continue
             for dx in (2, 1, 3, 0):
                 if dx == 0 and dy == 0:
                     continue
                 tx = up(x, dx, NX)
+                to_b, to_a = where_to(tx, ty)
                 remote(
-                    ybuf.at[r, ty, tx], summed.at[r, dy * NX + dx - 1], rs_send, rs_recv.at[r], device(x=tx, y=ty)
+                    ybuf.at[r, to_b, to_a], whole.at[dy * NX + dx - 1], whole_send, whole_recv, device(x=tx, y=ty)
                 ).start()
-
-    def send_home(r):
-        with scope("wrs"):
-            waits(summed.at[r], rs_recv.at[r])
-        acc = ybuf[r, y, x].astype(jnp.float32)
-        for s in range(PLANE - 1):
-            acc = acc + summed[r, s].astype(jnp.float32)
+        if not direct_sum:
+            for db in (2, 1, 3):
+                px, py = shifted(0, db)
+                remote(
+                    ybuf.at[r, up(my_b, db, NY)], half.at[r, db - 1], half_send, half_recv.at[r], device(x=px, y=py)
+                ).start()
+
+    def quarter_sum(r):
+        with scope("whalf"):
+            waits(half.at[r], half_recv.at[r])
+        for da in (2, 1, 3, 0):
+            a = up(my_a, da, NX)
+            acc = ybuf[r, my_b, a].astype(jnp.float32)
+            for k in range(NY - 1):
+                acc = acc + half[r, k, a].astype(jnp.float32)
+            ybuf[r, my_b, a] = acc.astype(jnp.bfloat16)
+            if da:
+                px, py = shifted(da, 0)
+                remote(
+                    ybuf.at[r, my_b, a], quarter.at[r, da - 1], quarter_send, quarter_recv.at[r], device(x=px, y=py)
+                ).start()
+
+    def send_home(r, direct_sum):
+        acc = ybuf[r, my_b, my_a].astype(jnp.float32)
+        if direct_sum:
+            with scope("wwhole"):
+                waits(whole, whole_recv)
+            for s in range(PLANE - 1):
+                acc = acc + whole[s].astype(jnp.float32)
+        else:
+            with scope("wquart"):
+                waits(quarter.at[r], quarter_recv.at[r])
+            for s in range(NX - 1):
+                acc = acc + quarter[r, s].astype(jnp.float32)
         total[...] = acc
         for s in range(NY):
             for h in range(2):
@@ -285,12 +347,11 @@
     with scope("wS0"):
         waits(gathered.at[order[0]], disp_recv.at[order[0]])
     with scope("S0"):
-        spread(order[0])
+        spread(order[0], True)
     @pl.when(c == 1)
     def _():
         lax.fori_loop(0, NY, to_region(ahead), 0)
         lax.fori_loop(0, NY, to_region(behind), 0)
-
     with scope("R"):
         @pl.when(relays & (zh == 3))
         def _():
@@ -303,66 +364,212 @@
         @pl.when(relays & (zh != 3))
         def _():
             second_leg(1, ahead, -6)
-
     for part, _, twin, _ in parts:
         remote(part, twin, twin_send, twin_recv, device(c=1 - c)).start()
-    with scope("wS1"):
-        waits(gathered.at[order[1]], disp_recv.at[order[1]])
-    with scope("S1"):
-        spread(order[1])
-    with scope("wtwin"):
-        waits(wraw.at[:, pl.ds(0, 3 * UNITS)], twin_recv)
-    for h in range(2):
-        wup[h, :, pl.ds(256, 256)] = wraw[h, pl.ds(256, 256), :].T
-    with scope("wS2"):
-        waits(gathered.at[order[2]], disp_recv.at[order[2]])
-    with scope("S2"):
-        spread(order[2])
+
     @pl.when(zh == 0)
     def _():
+        with scope("wS1"):
+            waits(gathered.at[order[1]], disp_recv.at[order[1]])
+        with scope("S1"):
+            spread(order[1], False)
+        with scope("wtwin"):
+            waits(wraw.at[:, pl.ds(0, 3 * UNITS)], twin_recv)
+        for h in range(2):
+            wup[h, :, pl.ds(256, 256)] = wraw[h, pl.ds(256, 256), :].T
+        with scope("wS2"):
+            waits(gathered.at[order[2]], disp_recv.at[order[2]])
+        with scope("S2"):
+            spread(order[2], False)
         with scope("A0"):
-            compute(work[0])
+            compute(work[0], True, False)
+        with scope("F1"):
+            pass_on(order[1])
         with scope("wS3"):
             waits(gathered.at[order[3]], disp_recv.at[order[3]])
         with scope("S3"):
-            spread(order[3])
+            spread(order[3], False)
+        with scope("F2"):
+            pass_on(order[2])
         with scope("A1"):
-            compute(work[1])
+            compute(work[1], False, False)
+        with scope("F3"):
+            pass_on(order[3])
         with scope("A2"):
-            compute(work[2])
+            compute(work[2], False, False)
+        with scope("Q0"):
+            quarter_sum(work[0])
+        with scope("Q1"):
+            quarter_sum(work[1])
+        with scope("A3"):
+            compute(work[3], False, True)
         with scope("Z0"):
-            send_home(work[0])
+            send_home(work[0], False)
+        with scope("Q2"):
+            quarter_sum(work[2])
+        with scope("Z1"):
+            send_home(work[1], False)
+        with scope("Z2"):
+            send_home(work[2], False)
+        with scope("Z3"):
+            send_home(work[3], True)
+
+    @pl.when(zh == 2)
+    def _():
+        with scope("wtwin"):
+            waits(wraw.at[:, pl.ds(0, 3 * UNITS)], twin_recv)
+        for h in range(2):
+            wup[h, :, pl.ds(256, 256)] = wraw[h, pl.ds(256, 256), :].T
+        with scope("wS2"):
+            waits(gathered.at[order[2]], disp_recv.at[order[2]])
+        with scope("S2"):
+            spread(order[2], True)
+        with scope("wS1"):
+            waits(gathered.at[order[1]], disp_recv.at[order[1]])
+        with scope("S1"):
+            spread(order[1], False)
+        with scope("A0"):
+            compute(work[0], True, True)
+        @pl.when(c == 0)
+        def _():
+            with scope("wS3"):
+                waits(gathered.at[order[3]], disp_recv.at[order[3]])
+            with scope("S3"):
+                spread(order[3], False)
+
+        @pl.when(c == 0)
+        def _():
+            with scope("F1"):
+                pass_on(order[1])
+
+        with scope("Z0"):
+            send_home(work[0], True)
+        @pl.when(c == 1)
+        def _():
+            with scope("wS3"):
+                waits(gathered.at[order[3]], disp_recv.at[order[3]])
+            with scope("S3"):
+                spread(order[3], False)
+
+        @pl.when(c == 1)
+        def _():
+            with scope("F1"):
+                pass_on(order[1])
+
+        with scope("F3"):
+            pass_on(order[3])
+        with scope("A1"):
+            compute(work[1], False, False)
         with scope("A3"):
-            compute(work[3])
+            compute(work[3], False, False)
+        with scope("Q1"):
+            quarter_sum(work[1])
         with scope("Z1"):
-            send_home(work[1])
+            send_home(work[1], False)
+        with scope("A2"):
+            compute(work[2], True, False)
+        with scope("Q3"):
+            quarter_sum(work[3])
+        with scope("Z3"):
+            send_home(work[3], False)
+        with scope("Q2"):
+            quarter_sum(work[2])
         with scope("Z2"):
-            send_home(work[2])
-        with scope("Z3"):
-            send_home(work[3])
-
-    @pl.when(zh != 0)
-    def _():
+            send_home(work[2], False)
+
+    @pl.when(zh == 1)
+    def _():
+        with scope("wS1"):
+            waits(gathered.at[order[1]], disp_recv.at[order[1]])
+        with scope("S1"):
+            spread(order[1], True)
+        with scope("wtwin"):
+            waits(wraw.at[:, pl.ds(0, 3 * UNITS)], twin_recv)
+        for h in range(2):
+            wup[h, :, pl.ds(256, 256)] = wraw[h, pl.ds(256, 256), :].T
         with scope("A0"):
-            compute(work[0])
+            compute(work[0], True, False)
+        with scope("wS2"):
+            waits(gathered.at[order[2]], disp_recv.at[order[2]])
+        with scope("S2"):
+            spread(order[2], False)
+        with scope("F2"):
+            pass_on(order[2])
+        with scope("A1"):
+            compute(work[1], True, True)
         with scope("wS3"):
             waits(gathered.at[order[3]], disp_recv.at[order[3]])
         with scope("S3"):
-            spread(order[3])
+            spread(order[3], False)
+        with scope("Q0"):
+            quarter_sum(work[0])
+        with scope("A2"):
+            compute(work[2], False, False)
+        with scope("F3"):
+            pass_on(order[3])
+        with scope("Z1"):
+            send_home(work[1], True)
+        with scope("Z0"):
+            send_home(work[0], False)
+        with scope("A3"):
+            compute(work[3], False, False)
+        with scope("Q2"):
+            quarter_sum(work[2])
+        with scope("Z2"):
+            send_home(work[2], False)
+        with scope("Q3"):
+            quarter_sum(work[3])
+        with scope("Z3"):
+            send_home(work[3], False)
+
+    @pl.when(zh == 3)
+    def _():
+        with scope("wS1"):
+            waits(gathered.at[order[1]], disp_recv.at[order[1]])
+        with scope("S1"):
+            spread(order[1], False)
+        with scope("wtwin"):
+            waits(wraw.at[:, pl.ds(0, 3 * UNITS)], twin_recv)
+        for h in range(2):
+            wup[h, :, pl.ds(256, 256)] = wraw[h, pl.ds(256, 256), :].T
+        with scope("A0"):
+            compute(work[0], True, False)
+        with scope("F1"):
+            pass_on(order[1])
+        with scope("wS2"):
+            waits(gathered.at[order[2]], disp_recv.at[order[2]])
+        with scope("S2"):
+            spread(order[2], False)
+        with scope("F2"):
+            pass_on(order[2])
         with scope("A1"):
-            compute(work[1])
+            compute(work[1], False, False)
+        with scope("wS3"):
+            waits(gathered.at[order[3]], disp_recv.at[order[3]])
+        with scope("S3"):
+            spread(order[3], False)
+        with scope("Q0"):
+            quarter_sum(work[0])
+        with scope("A2"):
+            compute(work[2], False, False)
+        with scope("F3"):
+            pass_on(order[3])
+        with scope("Q1"):
+            quarter_sum(work[1])
+        with scope("Z1"):
+            send_home(work[1], False)
+        with scope("A3"):
+            compute(work[3], False, False)
+        with scope("Q2"):
+            quarter_sum(work[2])
         with scope("Z0"):
-            send_home(work[0])
-        with scope("A2"):
-            compute(work[2])
-        with scope("Z1"):
-            send_home(work[1])
-        with scope("A3"):
-            compute(work[3])
+            send_home(work[0], False)
         with scope("Z2"):
-            send_home(work[2])
+            send_home(work[2], False)
+        with scope("Q3"):
+            quarter_sum(work[3])
         with scope("Z3"):
-            send_home(work[3])
+            send_home(work[3], False)
 
     with scope("wret"):
         waits(arrived, ret_recv)
@@ -394,7 +601,21 @@
 
         for r in range(NZH):
             waits(xbuf.at[r, :, :, pl.ds(0, (PLANE - 1) * LANES)], ag_send)
-            waits(summed.at[r], rs_send)
+        for r in range(NZH - 1):
+            waits(half.at[r], half_send)
+            waits(quarter.at[r], quarter_send)
+
+        whole_sum = (zh == 0) | (zh == 1) | (zh == 2)
+
+        @pl.when(jnp.logical_not(whole_sum))
+        def _():
+            waits(half.at[0], half_send)
+            waits(quarter.at[0], quarter_send)
+
+        @pl.when(whole_sum)
+        def _():
+            waits(whole, whole_send)
+
         waits(arrived.at[pl.ds(0, 3)], ret_send)
         waits(arrived.at[3, pl.ds(0, 7)], ret_send)
 
@@ -429,12 +650,15 @@
             pltpu.VMEM((NZH, NY, 2, PAIRS, 2, LANES), bf16),
             pltpu.VMEM((NZH, 2, ROWS, width // 2), bf16),
             pltpu.VMEM((NZH, NY, NX, 2, ROWS, LANES), bf16),
-            pltpu.VMEM((NZH, PLANE - 1, 2, ROWS, LANES), bf16),
+            pltpu.VMEM((NZH, NY - 1, NX, 2, ROWS, LANES), bf16),
+            pltpu.VMEM((NZH, NX - 1, 2, ROWS, LANES), bf16),
+            pltpu.VMEM((PLANE - 1, 2, ROWS, LANES), bf16),
             pltpu.VMEM((2, ROWS, LANES), f32),
             pltpu.VMEM((NZH, NY, 2, PAIRS, 2, LANES), bf16),
             pltpu.VMEM((NZH, NZL, PAIRS, 2, LANES), bf16),
             pltpu.VMEM((EXPERTS * SLOTS, LANES), f32),
-            dma((5,)), dma, dma, dma((2,)), dma, dma((4,)), dma, dma((4,)), dma, dma((4,)), dma, dma,
+            dma((5,)), dma, dma, dma((2,)), dma, dma((4,)), dma, dma((4, 2)),
+            dma, dma((4,)), dma, dma((4,)), dma, dma, dma, dma,
         ],
         compiler_params=pltpu.CompilerParams(
             collective_id=0, has_side_effects=True, vmem_limit_bytes=48 * 1024 * 1024

time: 71.2 us -> 68.7 us (0.965); the launches traced: 69.9 us -> 68.5 us
  Pallas kernels: 69.3 us -> 67.9 us
    pallas_call x1, Pallas kernels: 69.3 us -> 67.9 us  [local(): pl.pallas_call(moe_kernel, name='moe', out_shape=jax.ShapeDtypeStruct((to...]
where the time goes in v5:
time: 68.7 us; the launch traced here: 68.5 us
  Pallas kernels  67.9 us (99%)
    pallas_call x1, Pallas kernels, local(): pl.pallas_call(moe_kernel, name='moe', out_shape=jax.ShapeDtypeStruct((to...  67.9 us

profile of v5, /device:TPU:24, one launch (start us, length us, event | category | flops | bytes accessed | tf_op | source)
XLA Modules:
  0.0 68.5 jit_solution(15785299781385754555)
XLA Ops:
  0.0 67.9 %moe.1 = bf16[32,128]{1,0:T(8,128)(2,1)S(1)} custom-call(bf16[32,4096]{1,0:T(8,128)(2,1)} %hidden_any.1, s32[2,32]{1,0:T(2,128)} %bitcast.12, bf16[2,32]{1,0:T(2,128)(2,1)} %bitcast.13, bf16[112,4096]{1,0:T(8,128)(2,1)} %bitcast.9, bf16[112,4096]{1,0:T(8,128)(2,1)} %bitcast.10, bf16[112,4096]{1,0:T(8,128)(2,1)} %bitcast.11), custom_call_target="tpu_custom_call" | custom-call | tf_op jit(solution)/shard_map/moe/pallas_call | solution.py:635
  67.9 0.6 copy.8

commit v6 on v5

--- a/solution.py
+++ b/solution.py
@@ -24,7 +24,7 @@
     hidden_any, ids_any, gate_any, wg_any, wu_any, wd_any,
     out_ref,
     hid, ids_ref, gate_ref, wraw, wup, wdown, picked, passed, gathered, xbuf, ybuf, half, quarter, whole, total, homeward, arrived, returned,
-    load_sem, twin_send, twin_recv, leg_recv, disp_send, disp_recv, ag_send, ag_recv,
+    ready, load_sem, twin_send, twin_recv, leg_recv, disp_send, disp_recv, ag_send, ag_recv,
     half_send, half_recv, quarter_send, quarter_recv, whole_send, whole_recv, ret_send, ret_recv,
 ):
     scope = jax.named_scope
@@ -52,10 +52,12 @@
     def hello(**other):
         pl.semaphore_signal(barrier, inc=1, device_id=device(**other), device_id_type=MESH)
 
-    def hello_near(d, carry):
-        hello(y=up(y, d, NY), zh=ahead)
-        hello(y=up(y, d, NY), zh=behind)
-        return carry
+    def column(call, target):
+        def body(d, carry):
+            call(y=up(y, d, NY), zh=target)
+            return carry
+
+        lax.fori_loop(0, NY, body, 0)
 
     high, relays = zl >= NZL // 2, (zl >= 2) & (zl < 6)
 
@@ -75,7 +77,11 @@
         hello(x=up(x, lax.rem(p, NX), NX), y=up(y, p // NX, NY))
         return carry
 
-    lax.fori_loop(0, NY, hello_near, 0)
+    @pl.when(zh != 2)
+    def _():
+        column(hello, ahead)
+        column(hello, behind)
+
     lax.fori_loop(0, NY, hello_relay, 0)
 
     @pl.when(relays)
@@ -149,7 +155,7 @@
                 picked[k, j // 2, j % 2, p] = rows[16 * k + 2 * p : 16 * k + 2 * p + 2].astype(jnp.bfloat16)
 
     with scope("w_barrier"):
-        pl.semaphore_wait(barrier, 2 * NY + (NZL - 1) + (PLANE - 1) + 2 + jnp.where(relays, 2 * NY, 0))
+        pl.semaphore_wait(barrier, jnp.where(lax.rem(zh, 2) == 0, 2 * NY, NY) + (NZL - 1) + (PLANE - 1) + 2 + jnp.where(relays, 2 * NY, 0))
 
     order = (
         jnp.where(zh == 0, 0, jnp.where(zh == 1, 1, jnp.where(zh == 2, 2, 3))),
@@ -164,6 +170,14 @@
         jnp.where(zh == 0, 2, jnp.where(zh == 1, 3, jnp.where(zh == 2, 3, 2))),
     )
 
+    def say_ready(**other):
+        pl.semaphore_signal(ready, inc=1, device_id=device(**other), device_id_type=MESH)
+
+    @pl.when(zh == 2)
+    def _():
+        column(say_ready, ahead)
+        column(say_ready, behind)
+
     @pl.when(high)
     def _():
         remote(picked.at[1], passed.at[0], disp_send, leg_recv.at[0], device(**along(6))).start()
@@ -181,15 +195,12 @@
             return carry
         return send
 
-    @pl.when(c == 0)
-    def _():
-        lax.fori_loop(0, NY, to_region(jnp.where(high, ahead, behind)), 0)
-
     lax.fori_loop(1, NY, to_region(zh), 0)
     pltpu.make_async_copy(picked.at[0, y], gathered.at[zh, y], disp_recv.at[zh]).start()
 
     def second_leg(way, source, step):
-        waits(passed.at[way], leg_recv.at[way])
+        with scope("leg"):
+            waits(passed.at[way], leg_recv.at[way])
 
         def send(d, carry):
             ty = up(y, d, NY)
@@ -223,7 +234,8 @@
                     mine[h, pl.ds((s * PAIRS + p) * 2, 2), :] = gathered[r, s, h, p]
 
         def send_all(p, carry):
-            share(r, x, y, lax.rem(p, NX), p // NX, 1)
+            px, py = up(x, lax.rem(p, NX), NX), up(y, p // NX, NY)
+            remote(mine, mine, ag_send, ag_recv.at[r, 2 + p // NX], device(x=px, y=py)).start()
             return carry
 
         def send_axes(d, carry):
@@ -248,11 +260,28 @@
 
         lax.fori_loop(1, NX, take, 0)
 
-    def compute(r, direct, direct_sum):
-        with scope("wag"):
-            waits(xbuf.at[r, :, :, pl.ds(0, (PLANE - 1 if direct else PLANE - NX) * LANES)], ag_recv.at[r, 1])
-        up_gate = jnp.dot(xbuf[r, 0], wup[0], preferred_element_type=jnp.float32)
-        up_gate = up_gate + jnp.dot(xbuf[r, 1], wup[1], preferred_element_type=jnp.float32)
+    def halve(r):
+        for db in (2, 1, 3):
+            px, py = shifted(0, db)
+            remote(
+                ybuf.at[r, up(my_b, db, NY)], half.at[r, db - 1], half_send, half_recv.at[r], device(x=px, y=py)
+            ).start()
+
+    def compute(r, direct, direct_sum, hold=False):
+        if direct:
+            up_gate = None
+            for dy in (0, 1, 3, 2):
+                with scope("wag"):
+                    waits(xbuf.at[r, :, :, pl.ds(0, (NX if dy else NX - 1) * LANES)], ag_recv.at[r, 2 + dy])
+                row = pl.ds(pl.multiple_of(up(y, NY - dy, NY) * NX * LANES, NX * LANES), NX * LANES)
+                for h in range(2):
+                    part = jnp.dot(xbuf[r, h, :, row], wup[h, row, :], preferred_element_type=jnp.float32)
+                    up_gate = part if up_gate is None else up_gate + part
+        else:
+            with scope("wag"):
+                waits(xbuf.at[r, :, :, pl.ds(0, (PLANE - NX) * LANES)], ag_recv.at[r, 1])
+            up_gate = jnp.dot(xbuf[r, 0], wup[0], preferred_element_type=jnp.float32)
+            up_gate = up_gate + jnp.dot(xbuf[r, 1], wup[1], preferred_element_type=jnp.float32)
 
         def swish(k):
             g, u = up_gate[:, k * 256 : k * 256 + 128], up_gate[:, k * 256 + 128 : k * 256 + 256]
@@ -277,12 +306,8 @@
                 remote(
                     ybuf.at[r, to_b, to_a], whole.at[dy * NX + dx - 1], whole_send, whole_recv, device(x=tx, y=ty)
                 ).start()
-        if not direct_sum:
-            for db in (2, 1, 3):
-                px, py = shifted(0, db)
-                remote(
-                    ybuf.at[r, up(my_b, db, NY)], half.at[r, db - 1], half_send, half_recv.at[r], device(x=px, y=py)
-                ).start()
+        if not direct_sum and not hold:
+            halve(r)
 
     def quarter_sum(r):
         with scope("whalf"):
@@ -340,9 +365,17 @@
     for h in range(2):
         wup[h, :, pl.ds(0, 256)] = wraw[h, pl.ds(0, 256), :].T
 
-    @pl.when(c == 0)
+    @pl.when((c == 0) & (lax.rem(zh, 2) == 0))
+    def _():
+        lax.fori_loop(0, NY, to_region(jnp.where(high, ahead, behind)), 0)
+
+    @pl.when((c == 0) & (lax.rem(zh, 2) == 0))
     def _():
         lax.fori_loop(0, NY, to_region(jnp.where(high, behind, ahead)), 0)
+
+    @pl.when((c == 0) & (lax.rem(zh, 2) == 1))
+    def _():
+        lax.fori_loop(0, NY, to_region(0), 0)
 
     with scope("wS0"):
         waits(gathered.at[order[0]], disp_recv.at[order[0]])
@@ -350,8 +383,12 @@
         spread(order[0], True)
     @pl.when(c == 1)
     def _():
-        lax.fori_loop(0, NY, to_region(ahead), 0)
-        lax.fori_loop(0, NY, to_region(behind), 0)
+        lax.fori_loop(0, NY, to_region(jnp.where(lax.rem(zh, 2) == 0, ahead, 0)), 0)
+
+        @pl.when(lax.rem(zh, 2) == 0)
+        def _():
+            lax.fori_loop(0, NY, to_region(behind), 0)
+
     with scope("R"):
         @pl.when(relays & (zh == 3))
         def _():
@@ -437,11 +474,10 @@
             with scope("S3"):
                 spread(order[3], False)
 
-        @pl.when(c == 0)
-        def _():
-            with scope("F1"):
-                pass_on(order[1])
-
+        with scope("F1"):
+            pass_on(order[1])
+        with scope("A2"):
+            compute(work[2], True, False, True)
         with scope("Z0"):
             send_home(work[0], True)
         @pl.when(c == 1)
@@ -451,29 +487,40 @@
             with scope("S3"):
                 spread(order[3], False)
 
-        @pl.when(c == 1)
-        def _():
-            with scope("F1"):
-                pass_on(order[1])
-
-        with scope("F3"):
-            pass_on(order[3])
+        @pl.when(c == 0)
+        def _():
+            with scope("F3"):
+                pass_on(order[3])
+
         with scope("A1"):
             compute(work[1], False, False)
-        with scope("A3"):
-            compute(work[3], False, False)
+        @pl.when(c == 1)
+        def _():
+            with scope("F3"):
+                pass_on(order[3])
+
+        @pl.when(c == 0)
+        def _():
+            with scope("A3"):
+                compute(work[3], False, False)
+
+        with scope("H2"):
+            halve(work[2])
         with scope("Q1"):
             quarter_sum(work[1])
+        @pl.when(c == 1)
+        def _():
+            with scope("A3"):
+                compute(work[3], False, False)
+
         with scope("Z1"):
             send_home(work[1], False)
-        with scope("A2"):
-            compute(work[2], True, False)
         with scope("Q3"):
             quarter_sum(work[3])
+        with scope("Q2"):
+            quarter_sum(work[2])
         with scope("Z3"):
             send_home(work[3], False)
-        with scope("Q2"):
-            quarter_sum(work[2])
         with scope("Z2"):
             send_home(work[2], False)
 
@@ -483,6 +530,9 @@
             waits(gathered.at[order[1]], disp_recv.at[order[1]])
         with scope("S1"):
             spread(order[1], True)
+        with scope("NL"):
+            pl.semaphore_wait(ready, NY)
+        lax.fori_loop(0, NY, to_region(2), 0)
         with scope("wtwin"):
             waits(wraw.at[:, pl.ds(0, 3 * UNITS)], twin_recv)
         for h in range(2):
@@ -493,20 +543,20 @@
             waits(gathered.at[order[2]], disp_recv.at[order[2]])
         with scope("S2"):
             spread(order[2], False)
+        with scope("wS3"):
+            waits(gathered.at[order[3]], disp_recv.at[order[3]])
+        with scope("S3"):
+            spread(order[3], False)
         with scope("F2"):
             pass_on(order[2])
         with scope("A1"):
             compute(work[1], True, True)
-        with scope("wS3"):
-            waits(gathered.at[order[3]], disp_recv.at[order[3]])
-        with scope("S3"):
-            spread(order[3], False)
+        with scope("F3"):
+            pass_on(order[3])
         with scope("Q0"):
             quarter_sum(work[0])
         with scope("A2"):
             compute(work[2], False, False)
-        with scope("F3"):
-            pass_on(order[3])
         with scope("Z1"):
             send_home(work[1], True)
         with scope("Z0"):
@@ -528,6 +578,9 @@
             waits(gathered.at[order[1]], disp_recv.at[order[1]])
         with scope("S1"):
             spread(order[1], False)
+        with scope("NL"):
+            pl.semaphore_wait(ready, NY)
+        lax.fori_loop(0, NY, to_region(2), 0)
         with scope("wtwin"):
             waits(wraw.at[:, pl.ds(0, 3 * UNITS)], twin_recv)
         for h in range(2):
@@ -657,7 +710,7 @@
             pltpu.VMEM((NZH, NY, 2, PAIRS, 2, LANES), bf16),
             pltpu.VMEM((NZH, NZL, PAIRS, 2, LANES), bf16),
             pltpu.VMEM((EXPERTS * SLOTS, LANES), f32),
-            dma((5,)), dma, dma, dma((2,)), dma, dma((4,)), dma, dma((4, 2)),
+            pltpu.SemaphoreType.REGULAR, dma((5,)), dma, dma, dma((2,)), dma, dma((4,)), dma, dma((4, 2 + NY)),
             dma, dma((4,)), dma, dma((4,)), dma, dma, dma, dma,
         ],
         compiler_params=pltpu.CompilerParams(

time: 68.7 us -> 67.4 us (0.981)
  the two profiles are of different devices: /device:TPU:24 before, /device:TPU:256 now
where the time goes in v6:
time: 67.4 us; the launch traced here: 67.2 us
  Pallas kernels  66.6 us (99%)
    pallas_call x1, Pallas kernels, local(): pl.pallas_call(moe_kernel, name='moe', out_shape=jax.ShapeDtypeStruct((to...  66.6 us

profile of v6, /device:TPU:256, one launch (start us, length us, event | category | flops | bytes accessed | tf_op | source)
XLA Modules:
  0.0 67.2 jit_solution(641041167563318734)
XLA Ops:
  0.0 66.6 %moe.1 = bf16[32,128]{1,0:T(8,128)(2,1)S(1)} custom-call(bf16[32,4096]{1,0:T(8,128)(2,1)} %hidden_any.1, s32[2,32]{1,0:T(2,128)} %bitcast.12, bf16[2,32]{1,0:T(2,128)(2,1)} %bitcast.13, bf16[112,4096]{1,0:T(8,128)(2,1)} %bitcast.9, bf16[112,4096]{1,0:T(8,128)(2,1)} %bitcast.10, bf16[112,4096]{1,0:T(8,128)(2,1)} %bitcast.11), custom_call_target="tpu_custom_call" | custom-call | tf_op jit(solution)/shard_map/moe/pallas_call | solution.py:688
  66.6 0.6 copy.8

commit v7 on v6

--- a/solution.py
+++ b/solution.py
@@ -261,11 +261,14 @@
         lax.fori_loop(1, NX, take, 0)
 
     def halve(r):
-        for db in (2, 1, 3):
-            px, py = shifted(0, db)
-            remote(
-                ybuf.at[r, up(my_b, db, NY)], half.at[r, db - 1], half_send, half_recv.at[r], device(x=px, y=py)
-            ).start()
+        for da in (2, 1, 3, 0):
+            a = up(my_a, da, NX)
+            for db in (2, 1, 3):
+                px, py = shifted(0, db)
+                remote(
+                    ybuf.at[r, up(my_b, db, NY), a], half.at[r, db - 1, a], half_send, half_recv.at[r, da],
+                    device(x=px, y=py),
+                ).start()
 
     def compute(r, direct, direct_sum, hold=False):
         if direct:
@@ -310,10 +313,10 @@
             halve(r)
 
     def quarter_sum(r):
-        with scope("whalf"):
-            waits(half.at[r], half_recv.at[r])
         for da in (2, 1, 3, 0):
             a = up(my_a, da, NX)
+            with scope("whalf"):
+                waits(quarter.at[r], half_recv.at[r, da])
             acc = ybuf[r, my_b, a].astype(jnp.float32)
             for k in range(NY - 1):
                 acc = acc + half[r, k, a].astype(jnp.float32)
@@ -502,17 +505,22 @@
         @pl.when(c == 0)
         def _():
             with scope("A3"):
+                compute(work[3], False, False, True)
+
+        with scope("Q1"):
+            quarter_sum(work[1])
+        @pl.when(c == 0)
+        def _():
+            with scope("H3"):
+                halve(work[3])
+
+        @pl.when(c == 1)
+        def _():
+            with scope("A3"):
                 compute(work[3], False, False)
 
         with scope("H2"):
             halve(work[2])
-        with scope("Q1"):
-            quarter_sum(work[1])
-        @pl.when(c == 1)
-        def _():
-            with scope("A3"):
-                compute(work[3], False, False)
-
         with scope("Z1"):
             send_home(work[1], False)
         with scope("Q3"):
@@ -593,20 +601,20 @@
             waits(gathered.at[order[2]], disp_recv.at[order[2]])
         with scope("S2"):
             spread(order[2], False)
+        with scope("wS3"):
+            waits(gathered.at[order[3]], disp_recv.at[order[3]])
+        with scope("S3"):
+            spread(order[3], False)
         with scope("F2"):
             pass_on(order[2])
         with scope("A1"):
             compute(work[1], False, False)
-        with scope("wS3"):
-            waits(gathered.at[order[3]], disp_recv.at[order[3]])
-        with scope("S3"):
-            spread(order[3], False)
+        with scope("F3"):
+            pass_on(order[3])
         with scope("Q0"):
             quarter_sum(work[0])
         with scope("A2"):
             compute(work[2], False, False)
-        with scope("F3"):
-            pass_on(order[3])
         with scope("Q1"):
             quarter_sum(work[1])
         with scope("Z1"):
@@ -711,7 +719,7 @@
             pltpu.VMEM((NZH, NZL, PAIRS, 2, LANES), bf16),
             pltpu.VMEM((EXPERTS * SLOTS, LANES), f32),
             pltpu.SemaphoreType.REGULAR, dma((5,)), dma, dma, dma((2,)), dma, dma((4,)), dma, dma((4, 2 + NY)),
-            dma, dma((4,)), dma, dma((4,)), dma, dma, dma, dma,
+            dma, dma((4, NX)), dma, dma((4,)), dma, dma, dma, dma,
         ],
         compiler_params=pltpu.CompilerParams(
             collective_id=0, has_side_effects=True, vmem_limit_bytes=48 * 1024 * 1024

time: 67.4 us -> 66.7 us (0.990)
  the two profiles are of different devices: /device:TPU:256 before, /device:TPU:24 now
where the time goes in v7:
time: 66.7 us; the launch traced here: 66 us
  Pallas kernels  65.3 us (98%)
    pallas_call x1, Pallas kernels, local(): pl.pallas_call(moe_kernel, name='moe', out_shape=jax.ShapeDtypeStruct((to...  65.3 us

profile of v7, /device:TPU:24, one launch (start us, length us, event | category | flops | bytes accessed | tf_op | source)
XLA Modules:
  0.0 66.0 jit_solution(1575183638328884125)
XLA Ops:
  0.0 65.3 %moe.1 = bf16[32,128]{1,0:T(8,128)(2,1)S(1)} custom-call(bf16[32,4096]{1,0:T(8,128)(2,1)} %hidden_any.1, s32[2,32]{1,0:T(2,128)} %bitcast.12, bf16[2,32]{1,0:T(2,128)(2,1)} %bitcast.13, bf16[112,4096]{1,0:T(8,128)(2,1)} %bitcast.9, bf16[112,4096]{1,0:T(8,128)(2,1)} %bitcast.10, bf16[112,4096]{1,0:T(8,128)(2,1)} %bitcast.11), custom_call_target="tpu_custom_call" | custom-call | tf_op jit(solution)/shard_map/moe/pallas_call | solution.py:696
  65.4 0.6 copy.8

commit v8 on v7

--- a/solution.py
+++ b/solution.py
@@ -173,11 +173,6 @@
     def say_ready(**other):
         pl.semaphore_signal(ready, inc=1, device_id=device(**other), device_id_type=MESH)
 
-    @pl.when(zh == 2)
-    def _():
-        column(say_ready, ahead)
-        column(say_ready, behind)
-
     @pl.when(high)
     def _():
         remote(picked.at[1], passed.at[0], disp_send, leg_recv.at[0], device(**along(6))).start()
@@ -382,6 +377,11 @@
 
     with scope("wS0"):
         waits(gathered.at[order[0]], disp_recv.at[order[0]])
+    @pl.when(zh == 2)
+    def _():
+        column(say_ready, ahead)
+        column(say_ready, behind)
+
     with scope("S0"):
         spread(order[0], True)
     @pl.when(c == 1)
@@ -534,13 +534,13 @@
 
     @pl.when(zh == 1)
     def _():
+        with scope("NL"):
+            pl.semaphore_wait(ready, NY)
+        lax.fori_loop(0, NY, to_region(2), 0)
         with scope("wS1"):
             waits(gathered.at[order[1]], disp_recv.at[order[1]])
         with scope("S1"):
             spread(order[1], True)
-        with scope("NL"):
-            pl.semaphore_wait(ready, NY)
-        lax.fori_loop(0, NY, to_region(2), 0)
         with scope("wtwin"):
             waits(wraw.at[:, pl.ds(0, 3 * UNITS)], twin_recv)
         for h in range(2):
@@ -582,13 +582,13 @@
 
     @pl.when(zh == 3)
     def _():
+        with scope("NL"):
+            pl.semaphore_wait(ready, NY)
+        lax.fori_loop(0, NY, to_region(2), 0)
         with scope("wS1"):
             waits(gathered.at[order[1]], disp_recv.at[order[1]])
         with scope("S1"):
             spread(order[1], False)
-        with scope("NL"):
-            pl.semaphore_wait(ready, NY)
-        lax.fori_loop(0, NY, to_region(2), 0)
         with scope("wtwin"):
             waits(wraw.at[:, pl.ds(0, 3 * UNITS)], twin_recv)
         for h in range(2):

time: 66.7 us -> 66.4 us (level)
  no operation moved by 1% of the time
where the time goes in v8:
time: 66.4 us; the launch traced here: 66 us
  Pallas kernels  65.3 us (98%)
    pallas_call x1, Pallas kernels, local(): pl.pallas_call(moe_kernel, name='moe', out_shape=jax.ShapeDtypeStruct((to...  65.3 us

profile of v8, /device:TPU:24, one launch (start us, length us, event | category | flops | bytes accessed | tf_op | source)
XLA Modules:
  0.0 66.0 jit_solution(5597879525125931418)
XLA Ops:
  0.0 65.3 %moe.1 = bf16[32,128]{1,0:T(8,128)(2,1)S(1)} custom-call(bf16[32,4096]{1,0:T(8,128)(2,1)} %hidden_any.1, s32[2,32]{1,0:T(2,128)} %bitcast.12, bf16[2,32]{1,0:T(2,128)(2,1)} %bitcast.13, bf16[112,4096]{1,0:T(8,128)(2,1)} %bitcast.9, bf16[112,4096]{1,0:T(8,128)(2,1)} %bitcast.10, bf16[112,4096]{1,0:T(8,128)(2,1)} %bitcast.11), custom_call_target="tpu_custom_call" | custom-call | tf_op jit(solution)/shard_map/moe/pallas_call | solution.py:696
  65.4 0.6 copy.8
